TPU v7x, 512 devices: a whole 4x8x8 slice. The times are simulated.
512 devices in a mesh: lon: 64 (over y, z_hi, core), lat: 8 (over z_lo, x).
Axes of the slice: x: 4, y: 8, z: 8 (z_hi: 4, z_lo: 2; z = z_hi * 2 + z_lo), core: 2. Of those that a mesh axis runs over, the one named last changes fastest.
Arguments:
- target: float32 [3, 128, 65536], P(None, 'lat', 'lon'), may hold values from -6 to 6
- grad_x: float32 [2, 3, 128, 65536], P(None, None, 'lat', 'lon'), may hold values from -6 to 6
- grad_y: float32 [2, 3, 128, 65536], P(None, None, 'lat', 'lon'), may hold values from -6 to 6
- labels: int32 [128, 65536], P('lat', 'lon'), may hold values from 0 to 1
- sweeps: int32 [3], replicated, may hold values from 2 to 4
Outputs:
- stitched: float32 [3, 128, 65536], P(None, 'lat', 'lon')
All inputs are finite; a program needn't handle non-finite values.
Results may differ from a plain program's by a relative error of at most 0.0004.
Values sent between devices are 32-bit elements; how exact they have to be, the bound alone decides.
A program may use at most 64 MiB of HBM per device.

v0:
```python
import jax
import jax.numpy as jnp
from jax import lax
from jax.sharding import PartitionSpec as P

SOURCES = 2
LEVELS = 3
MAXS = 4


screening = 0.02
damping = 0.8


def with_halo(cells, sides, width, closed):
    for axis, dim in sides:
        count = lax.axis_size(axis)
        ends = count if closed else count - 1
        head = lax.slice_in_dim(cells, 0, width, axis=dim)
        tail = lax.slice_in_dim(cells, cells.shape[dim] - width, cells.shape[dim], axis=dim)
        cells = jnp.concatenate(
            [
                lax.ppermute(tail, axis, [(i, (i + 1) % count) for i in range(ends)]),
                cells,
                lax.ppermute(head, axis, [((i + 1) % count, i) for i in range(ends)]),
            ],
            axis=dim,
        )
    return cells


def shifted(block, axis, distance):
    devices = range(lax.axis_size(axis))
    route = [((i - distance) % len(devices), i) for i in devices]
    return lax.ppermute(block, axis, route)


def from_behind(value, axis, steps):
    count = lax.axis_size(axis)
    first, last = (max(0, -steps), min(count, count - steps))
    return lax.ppermute(value, axis, [(source, source + steps) for source in range(first, last)])


def extend(field, width):
    field = with_halo(field, (("lon", 2),), width, True)
    return with_halo(field, (("lat", 1),), width, False)


def stencil(padded, scale):
    inner = padded[:, 1:-1, 1:-1]
    beside = padded[:, :-2, 1:-1] + padded[:, 2:, 1:-1] + padded[:, 1:-1, :-2] + padded[:, 1:-1, 2:]
    return (screening + 4.0 * scale) * inner - scale * beside


def smooth(field, right, count, scale):
    diag = screening + 4.0 * scale
    rows = field.shape[1]
    both = extend(jnp.concatenate([field, right], 0), MAXS)
    value, wide_right = (both[:3], both[3:])
    first, total = (lax.axis_index("lat") * rows, rows * lax.axis_size("lat"))
    global_row = first - MAXS + lax.iota(jnp.int32, rows + 2 * MAXS)
    inside = ((global_row >= 0) & (global_row < total)).astype(jnp.float32)[None, :, None]

    def sweep_wide(step, value):
        padded = jnp.pad(value, ((0, 0), (1, 1), (1, 1)))
        return (value + damping * (wide_right - stencil(padded, scale)) / diag) * inside

    value = lax.fori_loop(0, count, sweep_wide, value)
    return value[:, MAXS:-MAXS, MAXS:-MAXS]


def restrict(field):
    chans, rows, cols = field.shape
    return field.reshape(chans, rows // 2, 2, cols // 2, 2).mean(axis=(2, 4))


def prolong_from(padded):
    center = padded[:, 1:-1, 1:-1]
    north = padded[:, :-2, 1:-1]
    south = padded[:, 2:, 1:-1]
    west = padded[:, 1:-1, :-2]
    east = padded[:, 1:-1, 2:]
    f00 = 0.5625 * center + 0.1875 * north + 0.1875 * west + 0.0625 * padded[:, :-2, :-2]
    f01 = 0.5625 * center + 0.1875 * north + 0.1875 * east + 0.0625 * padded[:, :-2, 2:]
    f10 = 0.5625 * center + 0.1875 * south + 0.1875 * west + 0.0625 * padded[:, 2:, :-2]
    f11 = 0.5625 * center + 0.1875 * south + 0.1875 * east + 0.0625 * padded[:, 2:, 2:]
    stacked = jnp.stack([jnp.stack([f00, f01], -1), jnp.stack([f10, f11], -1)], 2)
    chans, rows, two, cols, other = stacked.shape
    return stacked.reshape(chans, rows * 2, cols * 2)


def cycle(level, field, right, sweeps):
    scale = 0.25**level
    count = sweeps[level]
    field = smooth(field, right, count, scale)
    if level + 1 == LEVELS:
        return field
    resid = right - stencil(extend(field, 1), scale)
    coarse = restrict(resid)
    fix = cycle(level + 1, jnp.zeros_like(coarse), coarse, sweeps)
    field = field + prolong_from(extend(fix, 1))
    return smooth(field, right, count, scale)


def local(target, grad_x, grad_y, labels, sweeps):
    sel_x = jnp.zeros_like(target)
    sel_y = jnp.zeros_like(target)
    for source in range(SOURCES):
        picked = (labels == source)[None, :, :]
        sel_x = jnp.where(picked, grad_x[source], sel_x)
        sel_y = jnp.where(picked, grad_y[source], sel_y)
    west_col = shifted(sel_x[:, :, -1:], "lon", 1)
    north_row = from_behind(sel_y[:, -1:, :], "lat", 1)
    west = jnp.concatenate([west_col, sel_x[:, :, :-1]], axis=2)
    north = jnp.concatenate([north_row, sel_y[:, :-1, :]], axis=1)
    right = screening * target - (sel_x - west + (sel_y - north))
    return cycle(0, target, right, sweeps)


def solution(mesh):
    in_specs = (
        P(None, "lat", "lon"),
        P(None, None, "lat", "lon"),
        P(None, None, "lat", "lon"),
        P("lat", "lon"),
        P(),
    )
    out_specs = P(None, "lat", "lon")
    return jax.shard_map(local, mesh=mesh, in_specs=in_specs, out_specs=out_specs, check_vma=False)
```

profile of v0, /device:TPU:6, one launch (start us, length us, event | category | flops | bytes accessed | tf_op | source)
XLA Modules:
  0.0 282.4 jit_solution(16849004998563319617)
XLA Ops:
  2.2 4.2 %collective-permute-start.1 = (f32[3,1,1024]{2,1,0:T(1,128)S(1)}, f32[3,1,1024]{2,1,0:T(1,128)S(1)}, u32[]{:S(2)}, u32[]{:S(2)}) collective-permute-start(f32[3,1,1024]{2,1,0:T(1,128)S(1)} %slice.515), channel_id=1, source_target_pairs={{0,1},{1,2},{2,3},{3,4},{4,5},{5,6},{6,7},{8,9},{9,10},{10,11},{11... | collective-permute-start | bytes 36872 | tf_op jit(solution)/shard_map/ppermute | solution.py:41
  8.4 11.7 %collective-permute-done = f32[3,16,1]{2,1,0:T(8,128)S(1)} collective-permute-done((f32[3,16,1]{2,1,0:T(8,128)S(1)}, f32[3,16,1]{2,1,0:T(8,128)S(1)}, u32[]{:S(2)}, u32[]{:S(2)}) %collective-permute-start) | collective-permute-done | bytes 224 | tf_op jit(solution)/shard_map/ppermute | solution.py:35
  23.9 7.9 %collective-permute-start.3 = (f32[6,16,4]{2,1,0:T(8,128)S(1)}, f32[6,16,4]{2,1,0:T(8,128)S(1)}, u32[]{:S(2)}, u32[]{:S(2)}) collective-permute-start(f32[6,16,4]{2,1,0:T(8,128)S(1)} %get-tuple-element.485), channel_id=1, source_target_pairs={{8,0},{16,8},{24,16},{32,24},{40,32},{48,40},{56,48},{64,56},{72,6... | collective-permute-start | bytes 4616 | tf_op jit(solution)/shard_map/ppermute | solution.py:25
  33.8 3.6 %collective-permute-start.4 = (f32[6,4,1032]{2,1,0:T(4,128)S(1)}, f32[6,4,1032]{2,1,0:T(4,128)S(1)}, u32[]{:S(2)}, u32[]{:S(2)}) collective-permute-start(f32[6,4,1032]{2,1,0:T(4,128)S(1)} %get-tuple-element.481), channel_id=1, source_target_pairs={{0,1},{1,2},{2,3},{3,4},{4,5},{5,6},{6,7},{8,9},{9,10},{10,11},{11... | collective-permute-start | bytes 297224 | tf_op jit(solution)/shard_map/ppermute | solution.py:23
  37.5 2.2 collective-permute-start.5
  41.1 5.1 %collective-permute-done.5 = f32[6,4,1032]{2,1,0:T(4,128)S(1)} collective-permute-done((f32[6,4,1032]{2,1,0:T(4,128)S(1)}, f32[6,4,1032]{2,1,0:T(4,128)S(1)}, u32[]{:S(2)}, u32[]{:S(2)}) %collective-permute-start.5) | collective-permute-done | bytes 99104 | tf_op jit(solution)/shard_map/ppermute | solution.py:25
  46.4 2.5 while.65
  51.0 7.9 %collective-permute-start.7 = (f32[3,16,1]{2,1,0:T(8,128)S(1)}, f32[3,16,1]{2,1,0:T(8,128)S(1)}, u32[]{:S(2)}, u32[]{:S(2)}) collective-permute-start(f32[3,16,1]{2,1,0:T(8,128)S(1)} %get-tuple-element.488), channel_id=1, source_target_pairs={{8,0},{16,8},{24,16},{32,24},{40,32},{48,40},{56,48},{64,56},{72,6... | collective-permute-start | bytes 584 | tf_op jit(solution)/shard_map/ppermute | solution.py:25
  60.5 1.9 collective-permute-start.8
  62.5 3.9 %collective-permute-start.9 = (f32[3,1,1026]{2,1,0:T(1,128)S(1)}, f32[3,1,1026]{2,1,0:T(1,128)S(1)}, u32[]{:S(2)}, u32[]{:S(2)}) collective-permute-start(f32[3,1,1026]{2,1,0:T(1,128)S(1)} %get-tuple-element.494), channel_id=1, source_target_pairs={{1,0},{2,1},{3,2},{4,3},{5,4},{6,5},{7,6},{9,8},{10,9},{11,10},{12... | collective-permute-start | bytes 36944 | tf_op jit(solution)/shard_map/ppermute | solution.py:25
  66.4 3.8 %collective-permute-done.9 = f32[3,1,1026]{2,1,0:T(1,128)S(1)} collective-permute-done((f32[3,1,1026]{2,1,0:T(1,128)S(1)}, f32[3,1,1026]{2,1,0:T(1,128)S(1)}, u32[]{:S(2)}, u32[]{:S(2)}) %collective-permute-start.9) | collective-permute-done | bytes 12344 | tf_op jit(solution)/shard_map/ppermute | solution.py:25
  70.5 14.0 %reshape.71 = f32[3,8,2,512,2]{4,3,2,1,0:T(8,128)} reshape(f32[3,16,1024]{2,1,0:T(8,128)S(1)} %fusion.52) | data formatting | bytes 393216 | tf_op jit(solution)/shard_map/reshape | solution.py:74
  84.5 6.3 %reduce_sum.18 = f32[3,8,512]{2,1,0:T(8,128)S(1)} reduce(f32[3,8,2,512,2]{4,3,2,1,0:T(8,128)} %reshape.71, f32[]{:T(128)} %constant.174.clone.1), dimensions={2,4}, to_apply=%region_2.3 | reduce | flops 36864 | bytes 245764 | tf_op jit(solution)/shard_map/reduce_sum | solution.py:74
  92.8 7.9 %collective-permute-start.11 = (f32[6,8,4]{2,1,0:T(8,128)S(1)}, f32[6,8,4]{2,1,0:T(8,128)S(1)}, u32[]{:S(2)}, u32[]{:S(2)}) collective-permute-start(f32[6,8,4]{2,1,0:T(8,128)S(1)} %get-tuple-element.528), channel_id=1, source_target_pairs={{8,0},{16,8},{24,16},{32,24},{40,32},{48,40},{56,48},{64,56},{72,6... | collective-permute-start | bytes 2312 | tf_op jit(solution)/shard_map/ppermute | solution.py:25
  102.3 1.9 collective-permute-start.12
  104.3 3.9 %collective-permute-start.13 = (f32[6,4,520]{2,1,0:T(4,128)S(1)}, f32[6,4,520]{2,1,0:T(4,128)S(1)}, u32[]{:S(2)}, u32[]{:S(2)}) collective-permute-start(f32[6,4,520]{2,1,0:T(4,128)S(1)} %get-tuple-element.508), channel_id=1, source_target_pairs={{1,0},{2,1},{3,2},{4,3},{5,4},{6,5},{7,6},{9,8},{10,9},{11,10},{12... | collective-permute-start | bytes 149768 | tf_op jit(solution)/shard_map/ppermute | solution.py:25
  108.4 4.0 %collective-permute-done.13 = f32[6,4,520]{2,1,0:T(4,128)S(1)} collective-permute-done((f32[6,4,520]{2,1,0:T(4,128)S(1)}, f32[6,4,520]{2,1,0:T(4,128)S(1)}, u32[]{:S(2)}, u32[]{:S(2)}) %collective-permute-start.13) | collective-permute-done | bytes 49952 | tf_op jit(solution)/shard_map/ppermute | solution.py:25
  112.7 3.3 %while.66 = (s32[]{:T(128)}, f32[3,16,520]{2,1,0:T(8,128)S(1)}, s32[]{:T(128)}, f32[3,16,520]{2,1,0:T(8,128)S(1)}, s32[]{:T(128)}, /*index=5*/s32[]{:T(128)}) while((s32[]{:T(128)}, f32[3,16,520]{2,1,0:T(8,128)S(1)}, s32[]{:T(128)}, f32[3,16,520]{2,1,0:T(8,128)S(1)}, s32[]{:T(128)}, /*index=5*/s32[]{:T(128)}) %tuple.165), condition=%wide.region_4.5_spmd.clone, body=%wide.region_3.4_spmd.clone.sunk | while | flops 249682 | bytes 499401 | solution.py:68
  118.1 7.9 %collective-permute-start.15 = (f32[3,8,1]{2,1,0:T(8,128)S(1)}, f32[3,8,1]{2,1,0:T(8,128)S(1)}, u32[]{:S(2)}, u32[]{:S(2)}) collective-permute-start(f32[3,8,1]{2,1,0:T(8,128)S(1)} %get-tuple-element.506), channel_id=1, source_target_pairs={{8,0},{16,8},{24,16},{32,24},{40,32},{48,40},{56,48},{64,56},{72,6... | collective-permute-start | bytes 296 | tf_op jit(solution)/shard_map/ppermute | solution.py:25
  127.4 1.9 collective-permute-start.16
  129.4 3.9 %collective-permute-start.17 = (f32[3,1,514]{2,1,0:T(1,128)S(1)}, f32[3,1,514]{2,1,0:T(1,128)S(1)}, u32[]{:S(2)}, u32[]{:S(2)}) collective-permute-start(f32[3,1,514]{2,1,0:T(1,128)S(1)} %get-tuple-element.520), channel_id=1, source_target_pairs={{1,0},{2,1},{3,2},{4,3},{5,4},{6,5},{7,6},{9,8},{10,9},{11,10},{12... | collective-permute-start | bytes 18512 | tf_op jit(solution)/shard_map/ppermute | solution.py:25
  133.3 3.7 %collective-permute-done.17 = f32[3,1,514]{2,1,0:T(1,128)S(1)} collective-permute-done((f32[3,1,514]{2,1,0:T(1,128)S(1)}, f32[3,1,514]{2,1,0:T(1,128)S(1)}, u32[]{:S(2)}, u32[]{:S(2)}) %collective-permute-start.17) | collective-permute-done | bytes 6200 | tf_op jit(solution)/shard_map/ppermute | solution.py:25
  137.8 3.9 %reshape.72 = f32[3,4,2,256,2]{4,3,2,1,0:T(8,128)S(1)} reshape(f32[3,8,512]{2,1,0:T(8,128)} %fusion.78) | data formatting | bytes 98304 | tf_op jit(solution)/shard_map/reshape | solution.py:74
  144.2 7.9 %collective-permute-start.19 = (f32[6,4,4]{2,1,0:T(4,128)S(1)}, f32[6,4,4]{2,1,0:T(4,128)S(1)}, u32[]{:S(2)}, u32[]{:S(2)}) collective-permute-start(f32[6,4,4]{2,1,0:T(4,128)S(1)} %get-tuple-element.538), channel_id=1, source_target_pairs={{8,0},{16,8},{24,16},{32,24},{40,32},{48,40},{56,48},{64,56},{72,6... | collective-permute-start | bytes 1160 | tf_op jit(solution)/shard_map/ppermute | solution.py:25
  153.5 1.9 collective-permute-start.20
  155.4 3.9 %collective-permute-start.21 = (f32[6,4,264]{2,1,0:T(4,128)S(1)}, f32[6,4,264]{2,1,0:T(4,128)S(1)}, u32[]{:S(2)}, u32[]{:S(2)}) collective-permute-start(f32[6,4,264]{2,1,0:T(4,128)S(1)} %pad_maximum_fusion.26), channel_id=1, source_target_pairs={{1,0},{2,1},{3,2},{4,3},{5,4},{6,5},{7,6},{9,8},{10,9},{11,10},{12... | collective-permute-start | bytes 76040 | tf_op jit(solution)/shard_map/ppermute | solution.py:25
  159.4 4.0 %collective-permute-done.21 = f32[6,4,264]{2,1,0:T(4,128)S(1)} collective-permute-done((f32[6,4,264]{2,1,0:T(4,128)S(1)}, f32[6,4,264]{2,1,0:T(4,128)S(1)}, u32[]{:S(2)}, u32[]{:S(2)}) %collective-permute-start.21) | collective-permute-done | bytes 25376 | tf_op jit(solution)/shard_map/ppermute | solution.py:25
  163.6 2.2 while.67
  167.8 7.9 %collective-permute-start.23 = (f32[3,4,1]{2,1,0:T(4,128)S(1)}, f32[3,4,1]{2,1,0:T(4,128)S(1)}, u32[]{:S(2)}, u32[]{:S(2)}) collective-permute-start(f32[3,4,1]{2,1,0:T(4,128)S(1)} %get-tuple-element.518), channel_id=1, source_target_pairs={{8,0},{16,8},{24,16},{32,24},{40,32},{48,40},{56,48},{64,56},{72,6... | collective-permute-start | bytes 152 | tf_op jit(solution)/shard_map/ppermute | solution.py:25
  177.1 1.9 collective-permute-start.24
  179.0 4.1 %collective-permute-start.25 = (f32[3,1,258]{2,1,0:T(1,128)S(1)}, f32[3,1,258]{2,1,0:T(1,128)S(1)}, u32[]{:S(2)}, u32[]{:S(2)}) collective-permute-start(f32[3,1,258]{2,1,0:T(1,128)S(1)} %get-tuple-element.536), channel_id=1, source_target_pairs={{1,0},{2,1},{3,2},{4,3},{5,4},{6,5},{7,6},{9,8},{10,9},{11,10},{12... | collective-permute-start | bytes 9296 | tf_op jit(solution)/shard_map/ppermute | solution.py:25
  183.1 3.5 %collective-permute-done.25 = f32[3,1,258]{2,1,0:T(1,128)S(1)} collective-permute-done((f32[3,1,258]{2,1,0:T(1,128)S(1)}, f32[3,1,258]{2,1,0:T(1,128)S(1)}, u32[]{:S(2)}, u32[]{:S(2)}) %collective-permute-start.25) | collective-permute-done | bytes 3128 | tf_op jit(solution)/shard_map/ppermute | solution.py:25
  189.3 2.7 reshape.73
  195.0 7.9 %collective-permute-start.27 = (f32[6,8,4]{2,1,0:T(8,128)S(1)}, f32[6,8,4]{2,1,0:T(8,128)S(1)}, u32[]{:S(2)}, u32[]{:S(2)}) collective-permute-start(f32[6,8,4]{2,1,0:T(8,128)S(1)} %get-tuple-element.510), channel_id=1, source_target_pairs={{8,0},{16,8},{24,16},{32,24},{40,32},{48,40},{56,48},{64,56},{72,6... | collective-permute-start | bytes 2312 | tf_op jit(solution)/shard_map/ppermute | solution.py:25
  204.5 1.9 collective-permute-start.28
  206.4 3.9 %collective-permute-start.29 = (f32[6,4,520]{2,1,0:T(4,128)S(1)}, f32[6,4,520]{2,1,0:T(4,128)S(1)}, u32[]{:S(2)}, u32[]{:S(2)}) collective-permute-start(f32[6,4,520]{2,1,0:T(4,128)S(1)} %get-tuple-element.504), channel_id=1, source_target_pairs={{1,0},{2,1},{3,2},{4,3},{5,4},{6,5},{7,6},{9,8},{10,9},{11,10},{12... | collective-permute-start | bytes 149768 | tf_op jit(solution)/shard_map/ppermute | solution.py:25
  210.6 4.0 %collective-permute-done.29 = f32[6,4,520]{2,1,0:T(4,128)S(1)} collective-permute-done((f32[6,4,520]{2,1,0:T(4,128)S(1)}, f32[6,4,520]{2,1,0:T(4,128)S(1)}, u32[]{:S(2)}, u32[]{:S(2)}) %collective-permute-start.29) | collective-permute-done | bytes 49952 | tf_op jit(solution)/shard_map/ppermute | solution.py:25
  214.8 3.3 %while.68 = (s32[]{:T(128)}, f32[3,16,520]{2,1,0:T(8,128)S(1)}, s32[]{:T(128)}, f32[3,16,520]{2,1,0:T(8,128)S(1)}, s32[]{:T(128)}, /*index=5*/s32[]{:T(128)}) while((s32[]{:T(128)}, f32[3,16,520]{2,1,0:T(8,128)S(1)}, s32[]{:T(128)}, f32[3,16,520]{2,1,0:T(8,128)S(1)}, s32[]{:T(128)}, /*index=5*/s32[]{:T(128)}) %tuple.171), condition=%wide.region_9.10_spmd.clone, body=%wide.region_8.9_spmd.clone.sunk | while | flops 249682 | bytes 499401 | solution.py:68
  220.2 7.9 %collective-permute-start.31 = (f32[3,8,1]{2,1,0:T(8,128)S(1)}, f32[3,8,1]{2,1,0:T(8,128)S(1)}, u32[]{:S(2)}, u32[]{:S(2)}) collective-permute-start(f32[3,8,1]{2,1,0:T(8,128)S(1)} %get-tuple-element.502), channel_id=1, source_target_pairs={{8,0},{16,8},{24,16},{32,24},{40,32},{48,40},{56,48},{64,56},{72,6... | collective-permute-start | bytes 296 | tf_op jit(solution)/shard_map/ppermute | solution.py:25
  229.6 1.9 collective-permute-start.32
  231.5 3.9 %collective-permute-start.33 = (f32[3,1,514]{2,1,0:T(1,128)S(1)}, f32[3,1,514]{2,1,0:T(1,128)S(1)}, u32[]{:S(2)}, u32[]{:S(2)}) collective-permute-start(f32[3,1,514]{2,1,0:T(1,128)S(1)} %get-tuple-element.516), channel_id=1, source_target_pairs={{1,0},{2,1},{3,2},{4,3},{5,4},{6,5},{7,6},{9,8},{10,9},{11,10},{12... | collective-permute-start | bytes 18512 | tf_op jit(solution)/shard_map/ppermute | solution.py:25
  235.5 3.7 %collective-permute-done.33 = f32[3,1,514]{2,1,0:T(1,128)S(1)} collective-permute-done((f32[3,1,514]{2,1,0:T(1,128)S(1)}, f32[3,1,514]{2,1,0:T(1,128)S(1)}, u32[]{:S(2)}, u32[]{:S(2)}) %collective-permute-start.33) | collective-permute-done | bytes 6200 | tf_op jit(solution)/shard_map/ppermute | solution.py:25
  239.5 6.7 %copy.9 = f32[3,8,2,512,2]{4,3,2,1,0:T(8,128)} copy(f32[3,8,2,512,2]{3,1,0,4,2:T(8,128)S(1)} %pad_maximum_fusion.10) | data formatting | bytes 393216 | tf_op jit(solution)/shard_map/stack | solution.py:87
  246.3 9.8 %reshape.74 = f32[3,16,1024]{2,1,0:T(8,128)S(1)} reshape(f32[3,8,2,512,2]{4,3,2,1,0:T(8,128)} %copy.9) | data formatting | bytes 393216 | tf_op jit(solution)/shard_map/reshape | solution.py:89
  258.3 7.9 %collective-permute-start.35 = (f32[6,16,4]{2,1,0:T(8,128)S(1)}, f32[6,16,4]{2,1,0:T(8,128)S(1)}, u32[]{:S(2)}, u32[]{:S(2)}) collective-permute-start(f32[6,16,4]{2,1,0:T(8,128)S(1)} %get-tuple-element.483), channel_id=1, source_target_pairs={{8,0},{16,8},{24,16},{32,24},{40,32},{48,40},{56,48},{64,56},{72,6... | collective-permute-start | bytes 4616 | tf_op jit(solution)/shard_map/ppermute | solution.py:25
  270.1 3.9 %collective-permute-start.37 = (f32[6,4,1032]{2,1,0:T(4,128)S(1)}, f32[6,4,1032]{2,1,0:T(4,128)S(1)}, u32[]{:S(2)}, u32[]{:S(2)}) collective-permute-start(f32[6,4,1032]{2,1,0:T(4,128)S(1)} %get-tuple-element.480), channel_id=1, source_target_pairs={{1,0},{2,1},{3,2},{4,3},{5,4},{6,5},{7,6},{9,8},{10,9},{11,10},{12... | collective-permute-start | bytes 297224 | tf_op jit(solution)/shard_map/ppermute | solution.py:25
  274.8 4.0 %collective-permute-done.37 = f32[6,4,1032]{2,1,0:T(4,128)S(1)} collective-permute-done((f32[6,4,1032]{2,1,0:T(4,128)S(1)}, f32[6,4,1032]{2,1,0:T(4,128)S(1)}, u32[]{:S(2)}, u32[]{:S(2)}) %collective-permute-start.37) | collective-permute-done | bytes 99104 | tf_op jit(solution)/shard_map/ppermute | solution.py:25
  279.0 2.5 while.69
  (146 shorter events, 53.0 us)
Async XLA Ops:
  2.2 17.9 %collective-permute-start.1 = (f32[3,1,1024]{2,1,0:T(1,128)S(1)}, f32[3,1,1024]{2,1,0:T(1,128)S(1)}, u32[]{:S(2)}, u32[]{:S(2)}) collective-permute-start(f32[3,1,1024]{2,1,0:T(1,128)S(1)} %slice.515), channel_id=1, source_target_pairs={{0,1},{1,2},{2,3},{3,4},{4,5},{5,6},{6,7},{8,9},{9,10},{10,11},{11... | collective-permute-start | bytes 36872 | tf_op jit(solution)/shard_map/ppermute | solution.py:41
  6.4 13.6 %collective-permute-start = (f32[3,16,1]{2,1,0:T(8,128)S(1)}, f32[3,16,1]{2,1,0:T(8,128)S(1)}, u32[]{:S(2)}, u32[]{:S(2)}) collective-permute-start(f32[3,16,1]{2,1,0:T(8,128)S(1)} %slice.513), channel_id=1, source_target_pairs={{504,0},{0,8},{8,16},{16,24},{24,32},{32,40},{40,48},{48,56},{56,6... | collective-permute-start | bytes 584 | tf_op jit(solution)/shard_map/ppermute | solution.py:35
  21.1 63.4 %copy-start = (f32[3,16,1024]{2,1,0:T(8,128)}, f32[3,16,1024]{2,1,0:T(8,128)S(1)}, u32[]{:S(2)}) copy-start(f32[3,16,1024]{2,1,0:T(8,128)S(1)} %fusion.56) | copy-start | bytes 589828
  22.0 10.8 %collective-permute-start.2 = (f32[6,16,4]{2,1,0:T(8,128)S(1)}, f32[6,16,4]{2,1,0:T(8,128)S(1)}, u32[]{:S(2)}, u32[]{:S(2)}) collective-permute-start(f32[6,16,4]{2,1,0:T(8,128)S(1)} %get-tuple-element.486), channel_id=1, source_target_pairs={{0,8},{8,16},{16,24},{24,32},{32,40},{40,48},{48,56},{56,64},{64,7... | collective-permute-start | bytes 4616 | tf_op jit(solution)/shard_map/ppermute | solution.py:23
  23.9 9.6 %collective-permute-start.3 = (f32[6,16,4]{2,1,0:T(8,128)S(1)}, f32[6,16,4]{2,1,0:T(8,128)S(1)}, u32[]{:S(2)}, u32[]{:S(2)}) collective-permute-start(f32[6,16,4]{2,1,0:T(8,128)S(1)} %get-tuple-element.485), channel_id=1, source_target_pairs={{8,0},{16,8},{24,16},{32,24},{40,32},{48,40},{56,48},{64,56},{72,6... | collective-permute-start | bytes 4616 | tf_op jit(solution)/shard_map/ppermute | solution.py:25
  33.8 7.3 %collective-permute-start.4 = (f32[6,4,1032]{2,1,0:T(4,128)S(1)}, f32[6,4,1032]{2,1,0:T(4,128)S(1)}, u32[]{:S(2)}, u32[]{:S(2)}) collective-permute-start(f32[6,4,1032]{2,1,0:T(4,128)S(1)} %get-tuple-element.481), channel_id=1, source_target_pairs={{0,1},{1,2},{2,3},{3,4},{4,5},{5,6},{6,7},{8,9},{9,10},{10,11},{11... | collective-permute-start | bytes 297224 | tf_op jit(solution)/shard_map/ppermute | solution.py:23
  37.5 8.8 %collective-permute-start.5 = (f32[6,4,1032]{2,1,0:T(4,128)S(1)}, f32[6,4,1032]{2,1,0:T(4,128)S(1)}, u32[]{:S(2)}, u32[]{:S(2)}) collective-permute-start(f32[6,4,1032]{2,1,0:T(4,128)S(1)} %get-tuple-element.482), channel_id=1, source_target_pairs={{1,0},{2,1},{3,2},{4,3},{5,4},{6,5},{7,6},{9,8},{10,9},{11,10},{12... | collective-permute-start | bytes 297224 | tf_op jit(solution)/shard_map/ppermute | solution.py:25
  49.0 9.9 %collective-permute-start.6 = (f32[3,16,1]{2,1,0:T(8,128)S(1)}, f32[3,16,1]{2,1,0:T(8,128)S(1)}, u32[]{:S(2)}, u32[]{:S(2)}) collective-permute-start(f32[3,16,1]{2,1,0:T(8,128)S(1)} %get-tuple-element.487), channel_id=1, source_target_pairs={{0,8},{8,16},{16,24},{24,32},{32,40},{40,48},{48,56},{56,64},{64,7... | collective-permute-start | bytes 584 | tf_op jit(solution)/shard_map/ppermute | solution.py:23
  51.0 9.4 %collective-permute-start.7 = (f32[3,16,1]{2,1,0:T(8,128)S(1)}, f32[3,16,1]{2,1,0:T(8,128)S(1)}, u32[]{:S(2)}, u32[]{:S(2)}) collective-permute-start(f32[3,16,1]{2,1,0:T(8,128)S(1)} %get-tuple-element.488), channel_id=1, source_target_pairs={{8,0},{16,8},{24,16},{32,24},{40,32},{48,40},{56,48},{64,56},{72,6... | collective-permute-start | bytes 584 | tf_op jit(solution)/shard_map/ppermute | solution.py:25
  60.5 5.9 %collective-permute-start.8 = (f32[3,1,1026]{2,1,0:T(1,128)S(1)}, f32[3,1,1026]{2,1,0:T(1,128)S(1)}, u32[]{:S(2)}, u32[]{:S(2)}) collective-permute-start(f32[3,1,1026]{2,1,0:T(1,128)S(1)} %get-tuple-element.493), channel_id=1, source_target_pairs={{0,1},{1,2},{2,3},{3,4},{4,5},{5,6},{6,7},{8,9},{9,10},{10,11},{11... | collective-permute-start | bytes 36944 | tf_op jit(solution)/shard_map/ppermute | solution.py:23
  62.5 7.7 %collective-permute-start.9 = (f32[3,1,1026]{2,1,0:T(1,128)S(1)}, f32[3,1,1026]{2,1,0:T(1,128)S(1)}, u32[]{:S(2)}, u32[]{:S(2)}) collective-permute-start(f32[3,1,1026]{2,1,0:T(1,128)S(1)} %get-tuple-element.494), channel_id=1, source_target_pairs={{1,0},{2,1},{3,2},{4,3},{5,4},{6,5},{7,6},{9,8},{10,9},{11,10},{12... | collective-permute-start | bytes 36944 | tf_op jit(solution)/shard_map/ppermute | solution.py:25
  90.9 9.8 %collective-permute-start.10 = (f32[6,8,4]{2,1,0:T(8,128)S(1)}, f32[6,8,4]{2,1,0:T(8,128)S(1)}, u32[]{:S(2)}, u32[]{:S(2)}) collective-permute-start(f32[6,8,4]{2,1,0:T(8,128)S(1)} %get-tuple-element.527), channel_id=1, source_target_pairs={{0,8},{8,16},{16,24},{24,32},{32,40},{40,48},{48,56},{56,64},{64,7... | collective-permute-start | bytes 2312 | tf_op jit(solution)/shard_map/ppermute | solution.py:23
  92.8 9.4 %collective-permute-start.11 = (f32[6,8,4]{2,1,0:T(8,128)S(1)}, f32[6,8,4]{2,1,0:T(8,128)S(1)}, u32[]{:S(2)}, u32[]{:S(2)}) collective-permute-start(f32[6,8,4]{2,1,0:T(8,128)S(1)} %get-tuple-element.528), channel_id=1, source_target_pairs={{8,0},{16,8},{24,16},{32,24},{40,32},{48,40},{56,48},{64,56},{72,6... | collective-permute-start | bytes 2312 | tf_op jit(solution)/shard_map/ppermute | solution.py:25
  102.3 6.1 %collective-permute-start.12 = (f32[6,4,520]{2,1,0:T(4,128)S(1)}, f32[6,4,520]{2,1,0:T(4,128)S(1)}, u32[]{:S(2)}, u32[]{:S(2)}) collective-permute-start(f32[6,4,520]{2,1,0:T(4,128)S(1)} %get-tuple-element.507), channel_id=1, source_target_pairs={{0,1},{1,2},{2,3},{3,4},{4,5},{5,6},{6,7},{8,9},{9,10},{10,11},{11... | collective-permute-start | bytes 149768 | tf_op jit(solution)/shard_map/ppermute | solution.py:23
  104.3 8.2 %collective-permute-start.13 = (f32[6,4,520]{2,1,0:T(4,128)S(1)}, f32[6,4,520]{2,1,0:T(4,128)S(1)}, u32[]{:S(2)}, u32[]{:S(2)}) collective-permute-start(f32[6,4,520]{2,1,0:T(4,128)S(1)} %get-tuple-element.508), channel_id=1, source_target_pairs={{1,0},{2,1},{3,2},{4,3},{5,4},{6,5},{7,6},{9,8},{10,9},{11,10},{12... | collective-permute-start | bytes 149768 | tf_op jit(solution)/shard_map/ppermute | solution.py:25
  116.0 21.0 %copy-start.2 = (f32[3,16,520]{2,1,0:T(8,128)}, f32[3,16,520]{2,1,0:T(8,128)S(1)}, u32[]{:S(2)}) copy-start(f32[3,16,520]{2,1,0:T(8,128)S(1)} %get-tuple-element.351) | copy-start | bytes 299524
  116.2 9.8 %collective-permute-start.14 = (f32[3,8,1]{2,1,0:T(8,128)S(1)}, f32[3,8,1]{2,1,0:T(8,128)S(1)}, u32[]{:S(2)}, u32[]{:S(2)}) collective-permute-start(f32[3,8,1]{2,1,0:T(8,128)S(1)} %get-tuple-element.505), channel_id=1, source_target_pairs={{0,8},{8,16},{16,24},{24,32},{32,40},{40,48},{48,56},{56,64},{64,7... | collective-permute-start | bytes 296 | tf_op jit(solution)/shard_map/ppermute | solution.py:23
  118.1 9.3 %collective-permute-start.15 = (f32[3,8,1]{2,1,0:T(8,128)S(1)}, f32[3,8,1]{2,1,0:T(8,128)S(1)}, u32[]{:S(2)}, u32[]{:S(2)}) collective-permute-start(f32[3,8,1]{2,1,0:T(8,128)S(1)} %get-tuple-element.506), channel_id=1, source_target_pairs={{8,0},{16,8},{24,16},{32,24},{40,32},{48,40},{56,48},{64,56},{72,6... | collective-permute-start | bytes 296 | tf_op jit(solution)/shard_map/ppermute | solution.py:25
  127.4 5.9 %collective-permute-start.16 = (f32[3,1,514]{2,1,0:T(1,128)S(1)}, f32[3,1,514]{2,1,0:T(1,128)S(1)}, u32[]{:S(2)}, u32[]{:S(2)}) collective-permute-start(f32[3,1,514]{2,1,0:T(1,128)S(1)} %get-tuple-element.519), channel_id=1, source_target_pairs={{0,1},{1,2},{2,3},{3,4},{4,5},{5,6},{6,7},{8,9},{9,10},{10,11},{11... | collective-permute-start | bytes 18512 | tf_op jit(solution)/shard_map/ppermute | solution.py:23
  129.4 7.6 %collective-permute-start.17 = (f32[3,1,514]{2,1,0:T(1,128)S(1)}, f32[3,1,514]{2,1,0:T(1,128)S(1)}, u32[]{:S(2)}, u32[]{:S(2)}) collective-permute-start(f32[3,1,514]{2,1,0:T(1,128)S(1)} %get-tuple-element.520), channel_id=1, source_target_pairs={{1,0},{2,1},{3,2},{4,3},{5,4},{6,5},{7,6},{9,8},{10,9},{11,10},{12... | collective-permute-start | bytes 18512 | tf_op jit(solution)/shard_map/ppermute | solution.py:25
  142.2 9.8 %collective-permute-start.18 = (f32[6,4,4]{2,1,0:T(4,128)S(1)}, f32[6,4,4]{2,1,0:T(4,128)S(1)}, u32[]{:S(2)}, u32[]{:S(2)}) collective-permute-start(f32[6,4,4]{2,1,0:T(4,128)S(1)} %get-tuple-element.537), channel_id=1, source_target_pairs={{0,8},{8,16},{16,24},{24,32},{32,40},{40,48},{48,56},{56,64},{64,7... | collective-permute-start | bytes 1160 | tf_op jit(solution)/shard_map/ppermute | solution.py:23
  144.2 9.3 %collective-permute-start.19 = (f32[6,4,4]{2,1,0:T(4,128)S(1)}, f32[6,4,4]{2,1,0:T(4,128)S(1)}, u32[]{:S(2)}, u32[]{:S(2)}) collective-permute-start(f32[6,4,4]{2,1,0:T(4,128)S(1)} %get-tuple-element.538), channel_id=1, source_target_pairs={{8,0},{16,8},{24,16},{32,24},{40,32},{48,40},{56,48},{64,56},{72,6... | collective-permute-start | bytes 1160 | tf_op jit(solution)/shard_map/ppermute | solution.py:25
  153.5 5.9 %collective-permute-start.20 = (f32[6,4,264]{2,1,0:T(4,128)S(1)}, f32[6,4,264]{2,1,0:T(4,128)S(1)}, u32[]{:S(2)}, u32[]{:S(2)}) collective-permute-start(f32[6,4,264]{2,1,0:T(4,128)S(1)} %pad_maximum_fusion.26), channel_id=1, source_target_pairs={{0,1},{1,2},{2,3},{3,4},{4,5},{5,6},{6,7},{8,9},{9,10},{10,11},{11... | collective-permute-start | bytes 76040 | tf_op jit(solution)/shard_map/ppermute | solution.py:23
  155.4 8.0 %collective-permute-start.21 = (f32[6,4,264]{2,1,0:T(4,128)S(1)}, f32[6,4,264]{2,1,0:T(4,128)S(1)}, u32[]{:S(2)}, u32[]{:S(2)}) collective-permute-start(f32[6,4,264]{2,1,0:T(4,128)S(1)} %pad_maximum_fusion.26), channel_id=1, source_target_pairs={{1,0},{2,1},{3,2},{4,3},{5,4},{6,5},{7,6},{9,8},{10,9},{11,10},{12... | collective-permute-start | bytes 76040 | tf_op jit(solution)/shard_map/ppermute | solution.py:25
  165.9 9.8 %collective-permute-start.22 = (f32[3,4,1]{2,1,0:T(4,128)S(1)}, f32[3,4,1]{2,1,0:T(4,128)S(1)}, u32[]{:S(2)}, u32[]{:S(2)}) collective-permute-start(f32[3,4,1]{2,1,0:T(4,128)S(1)} %get-tuple-element.517), channel_id=1, source_target_pairs={{0,8},{8,16},{16,24},{24,32},{32,40},{40,48},{48,56},{56,64},{64,7... | collective-permute-start | bytes 152 | tf_op jit(solution)/shard_map/ppermute | solution.py:23
  167.8 9.2 %collective-permute-start.23 = (f32[3,4,1]{2,1,0:T(4,128)S(1)}, f32[3,4,1]{2,1,0:T(4,128)S(1)}, u32[]{:S(2)}, u32[]{:S(2)}) collective-permute-start(f32[3,4,1]{2,1,0:T(4,128)S(1)} %get-tuple-element.518), channel_id=1, source_target_pairs={{8,0},{16,8},{24,16},{32,24},{40,32},{48,40},{56,48},{64,56},{72,6... | collective-permute-start | bytes 152 | tf_op jit(solution)/shard_map/ppermute | solution.py:25
  177.1 6.0 %collective-permute-start.24 = (f32[3,1,258]{2,1,0:T(1,128)S(1)}, f32[3,1,258]{2,1,0:T(1,128)S(1)}, u32[]{:S(2)}, u32[]{:S(2)}) collective-permute-start(f32[3,1,258]{2,1,0:T(1,128)S(1)} %get-tuple-element.535), channel_id=1, source_target_pairs={{0,1},{1,2},{2,3},{3,4},{4,5},{5,6},{6,7},{8,9},{9,10},{10,11},{11... | collective-permute-start | bytes 9296 | tf_op jit(solution)/shard_map/ppermute | solution.py:23
  179.0 7.6 %collective-permute-start.25 = (f32[3,1,258]{2,1,0:T(1,128)S(1)}, f32[3,1,258]{2,1,0:T(1,128)S(1)}, u32[]{:S(2)}, u32[]{:S(2)}) collective-permute-start(f32[3,1,258]{2,1,0:T(1,128)S(1)} %get-tuple-element.536), channel_id=1, source_target_pairs={{1,0},{2,1},{3,2},{4,3},{5,4},{6,5},{7,6},{9,8},{10,9},{11,10},{12... | collective-permute-start | bytes 9296 | tf_op jit(solution)/shard_map/ppermute | solution.py:25
  193.1 9.8 %collective-permute-start.26 = (f32[6,8,4]{2,1,0:T(8,128)S(1)}, f32[6,8,4]{2,1,0:T(8,128)S(1)}, u32[]{:S(2)}, u32[]{:S(2)}) collective-permute-start(f32[6,8,4]{2,1,0:T(8,128)S(1)} %get-tuple-element.509), channel_id=1, source_target_pairs={{0,8},{8,16},{16,24},{24,32},{32,40},{40,48},{48,56},{56,64},{64,7... | collective-permute-start | bytes 2312 | tf_op jit(solution)/shard_map/ppermute | solution.py:23
  195.0 9.4 %collective-permute-start.27 = (f32[6,8,4]{2,1,0:T(8,128)S(1)}, f32[6,8,4]{2,1,0:T(8,128)S(1)}, u32[]{:S(2)}, u32[]{:S(2)}) collective-permute-start(f32[6,8,4]{2,1,0:T(8,128)S(1)} %get-tuple-element.510), channel_id=1, source_target_pairs={{8,0},{16,8},{24,16},{32,24},{40,32},{48,40},{56,48},{64,56},{72,6... | collective-permute-start | bytes 2312 | tf_op jit(solution)/shard_map/ppermute | solution.py:25
  204.5 6.1 %collective-permute-start.28 = (f32[6,4,520]{2,1,0:T(4,128)S(1)}, f32[6,4,520]{2,1,0:T(4,128)S(1)}, u32[]{:S(2)}, u32[]{:S(2)}) collective-permute-start(f32[6,4,520]{2,1,0:T(4,128)S(1)} %get-tuple-element.503), channel_id=1, source_target_pairs={{0,1},{1,2},{2,3},{3,4},{4,5},{5,6},{6,7},{8,9},{9,10},{10,11},{11... | collective-permute-start | bytes 149768 | tf_op jit(solution)/shard_map/ppermute | solution.py:23
  206.4 8.2 %collective-permute-start.29 = (f32[6,4,520]{2,1,0:T(4,128)S(1)}, f32[6,4,520]{2,1,0:T(4,128)S(1)}, u32[]{:S(2)}, u32[]{:S(2)}) collective-permute-start(f32[6,4,520]{2,1,0:T(4,128)S(1)} %get-tuple-element.504), channel_id=1, source_target_pairs={{1,0},{2,1},{3,2},{4,3},{5,4},{6,5},{7,6},{9,8},{10,9},{11,10},{12... | collective-permute-start | bytes 149768 | tf_op jit(solution)/shard_map/ppermute | solution.py:25
  218.3 9.8 %collective-permute-start.30 = (f32[3,8,1]{2,1,0:T(8,128)S(1)}, f32[3,8,1]{2,1,0:T(8,128)S(1)}, u32[]{:S(2)}, u32[]{:S(2)}) collective-permute-start(f32[3,8,1]{2,1,0:T(8,128)S(1)} %get-tuple-element.501), channel_id=1, source_target_pairs={{0,8},{8,16},{16,24},{24,32},{32,40},{40,48},{48,56},{56,64},{64,7... | collective-permute-start | bytes 296 | tf_op jit(solution)/shard_map/ppermute | solution.py:23
  220.2 9.3 %collective-permute-start.31 = (f32[3,8,1]{2,1,0:T(8,128)S(1)}, f32[3,8,1]{2,1,0:T(8,128)S(1)}, u32[]{:S(2)}, u32[]{:S(2)}) collective-permute-start(f32[3,8,1]{2,1,0:T(8,128)S(1)} %get-tuple-element.502), channel_id=1, source_target_pairs={{8,0},{16,8},{24,16},{32,24},{40,32},{48,40},{56,48},{64,56},{72,6... | collective-permute-start | bytes 296 | tf_op jit(solution)/shard_map/ppermute | solution.py:25
  229.6 5.9 %collective-permute-start.32 = (f32[3,1,514]{2,1,0:T(1,128)S(1)}, f32[3,1,514]{2,1,0:T(1,128)S(1)}, u32[]{:S(2)}, u32[]{:S(2)}) collective-permute-start(f32[3,1,514]{2,1,0:T(1,128)S(1)} %get-tuple-element.515), channel_id=1, source_target_pairs={{0,1},{1,2},{2,3},{3,4},{4,5},{5,6},{6,7},{8,9},{9,10},{10,11},{11... | collective-permute-start | bytes 18512 | tf_op jit(solution)/shard_map/ppermute | solution.py:23
  231.5 7.6 %collective-permute-start.33 = (f32[3,1,514]{2,1,0:T(1,128)S(1)}, f32[3,1,514]{2,1,0:T(1,128)S(1)}, u32[]{:S(2)}, u32[]{:S(2)}) collective-permute-start(f32[3,1,514]{2,1,0:T(1,128)S(1)} %get-tuple-element.516), channel_id=1, source_target_pairs={{1,0},{2,1},{3,2},{4,3},{5,4},{6,5},{7,6},{9,8},{10,9},{11,10},{12... | collective-permute-start | bytes 18512 | tf_op jit(solution)/shard_map/ppermute | solution.py:25
  239.5 16.7 %copy-start.1 = (f32[3,16,1024]{2,1,0:T(8,128)S(1)}, f32[3,16,1024]{2,1,0:T(8,128)}, u32[]{:S(2)}) copy-start(f32[3,16,1024]{2,1,0:T(8,128)} %copy-done) | copy-start | bytes 589828
  256.3 9.8 %collective-permute-start.34 = (f32[6,16,4]{2,1,0:T(8,128)S(1)}, f32[6,16,4]{2,1,0:T(8,128)S(1)}, u32[]{:S(2)}, u32[]{:S(2)}) collective-permute-start(f32[6,16,4]{2,1,0:T(8,128)S(1)} %get-tuple-element.484), channel_id=1, source_target_pairs={{0,8},{8,16},{16,24},{24,32},{32,40},{40,48},{48,56},{56,64},{64,7... | collective-permute-start | bytes 4616 | tf_op jit(solution)/shard_map/ppermute | solution.py:23
  258.3 9.6 %collective-permute-start.35 = (f32[6,16,4]{2,1,0:T(8,128)S(1)}, f32[6,16,4]{2,1,0:T(8,128)S(1)}, u32[]{:S(2)}, u32[]{:S(2)}) collective-permute-start(f32[6,16,4]{2,1,0:T(8,128)S(1)} %get-tuple-element.483), channel_id=1, source_target_pairs={{8,0},{16,8},{24,16},{32,24},{40,32},{48,40},{56,48},{64,56},{72,6... | collective-permute-start | bytes 4616 | tf_op jit(solution)/shard_map/ppermute | solution.py:25
  268.2 6.6 %collective-permute-start.36 = (f32[6,4,1032]{2,1,0:T(4,128)S(1)}, f32[6,4,1032]{2,1,0:T(4,128)S(1)}, u32[]{:S(2)}, u32[]{:S(2)}) collective-permute-start(f32[6,4,1032]{2,1,0:T(4,128)S(1)} %get-tuple-element.479), channel_id=1, source_target_pairs={{0,1},{1,2},{2,3},{3,4},{4,5},{5,6},{6,7},{8,9},{9,10},{10,11},{11... | collective-permute-start | bytes 297224 | tf_op jit(solution)/shard_map/ppermute | solution.py:23
  270.1 8.8 %collective-permute-start.37 = (f32[6,4,1032]{2,1,0:T(4,128)S(1)}, f32[6,4,1032]{2,1,0:T(4,128)S(1)}, u32[]{:S(2)}, u32[]{:S(2)}) collective-permute-start(f32[6,4,1032]{2,1,0:T(4,128)S(1)} %get-tuple-element.480), channel_id=1, source_target_pairs={{1,0},{2,1},{3,2},{4,3},{5,4},{6,5},{7,6},{9,8},{10,9},{11,10},{12... | collective-permute-start | bytes 297224 | tf_op jit(solution)/shard_map/ppermute | solution.py:25
where the time goes:
time: 286 us; the launch traced here: 282 us
  starting transfers between devices  147 us (51%)
  waiting for transfers between devices  61.1 us (21%)
  local copies, waits for them, and re-layouts  43.2 us (15%)
  other arithmetic  18.7 us (7%)
  loops' own time  11.6 us (4%)
    ppermute x18, starting transfers between devices, with_halo(): lax.ppermute(head, axis, [((i + 1) % count, i) for i in range(ends)])  105 us
    ppermute x18, waiting for transfers between devices, with_halo(): lax.ppermute(head, axis, [((i + 1) % count, i) for i in range(ends)])  48.1 us
    ppermute x18, starting transfers between devices, with_halo(): lax.ppermute(tail, axis, [(i, (i + 1) % count) for i in range(ends)])  36.2 us
    reshape x2, local copies, waits for them, and re-layouts, restrict(): return field.reshape(chans, rows // 2, 2, cols // 2, 2).mean(axis=(2, 4))  17.9 us
    reshape x2, local copies, waits for them, and re-layouts, prolong_from(): return stacked.reshape(chans, rows * 2, cols * 2)  12.6 us
    ppermute x1, waiting for transfers between devices, shifted(): return lax.ppermute(block, axis, route)  11.7 us
    another operation x5, loops' own time, smooth(): value = lax.fori_loop(0, count, sweep_wide, value)  11.6 us
    another operation x2, local copies, waits for them, and re-layouts, prolong_from(): jnp.stack([jnp.stack([f00, f01], -1), jnp.stack([f10, f11], -1)], 2)  8.5 us
  transfers between devices with their start and end apart: 38, of which 22 were waited for; matrix products, arithmetic and copies ran while one was open for 1% of the time, Pallas kernels for 0%

commit v1 on v0

v1 whole, which is shorter than its diff:
```python
import functools

import jax
import jax.numpy as jnp
from jax import lax
from jax.experimental import pallas as pl
from jax.experimental.pallas import tpu as pltpu
from jax.sharding import PartitionSpec as P

SOURCES = 2
LEVELS = 3
MAXS = 4
CH = 3
ROWS = 16
TILES = 8
L = 128

screening = 0.02
damping = 0.8
MESH = pl.DeviceIdType.MESH

T0, T1, T2 = TILES + 1, TILES // 2 + 1, TILES // 4 + 1
R0 = 24
R1 = 56
R2 = 24
RP = 24


def iota(rows, dim):
    return lax.broadcasted_iota(jnp.int32, (rows, L), dim)


def lanes_of(rows):
    lane = iota(rows, 1)
    return lane == 0, lane == L - 1, lane < L // 2


def up(x):
    return pltpu.roll(x, x.shape[0] - 1, 0)


def down(x):
    return pltpu.roll(x, 1, 0)


def left(x):
    return pltpu.roll(x, L - 1, 1)


def right(x):
    return pltpu.roll(x, 1, 1)


def beside(xs, first, last):
    rights = [right(x) for x in xs]
    lefts = [left(x) for x in xs]
    count = len(xs)
    sums = []
    for t, x in enumerate(xs):
        west = jnp.where(first, rights[t - 1], rights[t])
        east = jnp.where(last, lefts[(t + 1) % count], lefts[t])
        sums.append((up(x) + down(x)) + (west + east))
    return sums


def sweep(src, dst, rhs, tiles, rows, base, factor, scale):
    diag = screening + 4.0 * scale
    first, last, _ = lanes_of(rows)

    def body(c, carry):
        xs = [src[c, t] for t in range(tiles)]
        sums = beside(xs, first, last)
        for t in range(tiles):
            b = rhs[c, t, base : base + rows]
            dst[c, t] = xs[t] + factor * ((b - diag * xs[t]) + scale * sums[t])
        return carry

    lax.fori_loop(0, CH, body, 0)


def restrict(src, rhs, dst, dst_base, tmp, tiles, rows, start, count, scale):
    diag = screening + 4.0 * scale
    first, last, _ = lanes_of(rows)
    low = lanes_of(count)[2]
    pick = (2 * iota(count, 1)) % L

    def body(c, carry):
        xs = [src[c, t] for t in range(tiles)]
        sums = beside(xs, first, last)
        for t in range(tiles):
            tmp[t, 0:rows] = (rhs[c, t, 0:rows] - diag * xs[t]) + scale * sums[t]
        parts = []
        for t in range(tiles):
            pair = tmp[t, pl.ds(start, count, stride=2)] + tmp[t, pl.ds(start + 1, count, stride=2)]
            pair = pair + left(pair)
            parts.append(0.25 * jnp.take_along_axis(pair, pick, axis=1))
        for t in range(tiles // 2):
            dst[c, t, dst_base : dst_base + count] = jnp.where(low, parts[2 * t], parts[2 * t + 1])
        dst[c, tiles // 2, dst_base : dst_base + count] = parts[-1]
        return carry

    lax.fori_loop(0, CH, body, 0)


def prolong_rows(src, c, tiles, rows, tmp):
    for t in range(tiles):
        x = src[c, t]
        tmp[t, pl.ds(0, rows, stride=2)] = 0.75 * x + 0.25 * down(x)
        tmp[t, pl.ds(1, rows, stride=2)] = 0.75 * x + 0.25 * up(x)


def prolong_cols(xs, rows):
    lane = iota(rows, 1)
    first, last, low = lanes_of(rows)
    aside = jnp.where(lane % 2 == 0, L - 1, 1)
    count = len(xs)
    out = []
    for t in range(count):
        wests = right(xs[t - 1])
        easts = left(xs[(t + 1) % count])
        for h in range(2 if t < count - 1 else 1):
            here = lane // 2 + (h * (L // 2) if t < count - 1 else jnp.where(low, 0, L // 2))
            near = jnp.take_along_axis(xs[t], here, axis=1)
            far = jnp.take_along_axis(xs[t], (here + aside) % L, axis=1)
            if h == 0:
                far = jnp.where(first, wests, far)
            if h == 1 or t == count - 1:
                far = jnp.where(last, easts, far)
            out.append(0.75 * near + 0.25 * far)
    return out


def kernel(
    sweeps, target, grad_x, grad_y, labels, out,
    gx, gy, lab, v0, w0, b0, sx, wx, sy, ny, ps, pn, rn, rs, re, rw,
    b1, v1, w1, vp, wp, b2, v2, w2, zn, zs, tmp,
    in_sem, send, recv,
):
    lon, lat = lax.axis_index("lon"), lax.axis_index("lat")
    nlon, nlat = lax.axis_size("lon"), lax.axis_size("lat")

    def peer(dlat, dlon):
        return {"lat": lax.rem(lat + dlat + nlat, nlat), "lon": lax.rem(lon + dlon + nlon, nlon)}

    loads = [
        pltpu.make_async_copy(labels, lab, in_sem.at[0]),
        pltpu.make_async_copy(grad_x, gx, in_sem.at[1]),
        pltpu.make_async_copy(grad_y, gy, in_sem.at[2]),
    ]
    for t in range(TILES):
        loads.append(
            pltpu.make_async_copy(
                target.at[:, :, pl.ds(t * L, L)], v0.at[:, t, pl.ds(0, ROWS)], in_sem.at[3 + t]
            )
        )
    for load in loads:
        load.start()

    peers = [(d, 0) for d in (1, -1, 2, -2, 3, -3)]
    peers += [(i, j) for i in (-1, 0, 1) for j in (-1, 1)]
    barrier = pltpu.get_barrier_semaphore()
    for dlat, dlon in peers:
        pl.semaphore_signal(barrier, inc=1, device_id=peer(dlat, dlon), device_id_type=MESH)

    used = [0]

    def remote(src, dst, dlat, dlon):
        k = used[0]
        used[0] += 1
        return pltpu.make_async_remote_copy(
            src_ref=src,
            dst_ref=dst,
            send_sem=send.at[k],
            recv_sem=recv.at[k],
            device_id=peer(dlat, dlon),
            device_id_type=MESH,
        )

    first, last, low = lanes_of(ROWS)
    first8, last8, low8 = lanes_of(8)
    sub8 = iota(8, 0)
    north_half = sub8 < 4
    row16 = iota(ROWS, 0)

    def factors(level, rows, total, at):
        diag = screening + 4.0 * 0.25**level
        here = iota(rows, 0)
        here = at(here) + lat * (ROWS >> level)
        inside = jnp.where((here >= 0) & (here < total), 1.0, 0.0).astype(jnp.float32)
        steps = [
            jnp.where(sweeps[level] > i, damping / diag, 0.0).astype(jnp.float32) for i in range(MAXS)
        ]
        return inside, [inside * step for step in steps]

    for load in loads[:3]:
        load.wait()

    def picked(ref, c, t, rows):
        cols = slice(t * L, (t + 1) * L)
        return jnp.where(lab[rows, cols] == 0, ref[0, c, rows, cols], ref[1, c, rows, cols])

    for c in range(CH):
        sx[c] = picked(gx, c, TILES - 1, slice(0, ROWS))
    for t in range(TILES):
        edge = [pltpu.roll(picked(gy, c, t, slice(8, 16)), c + 1, 0) for c in range(CH)]
        sy[t] = jnp.where(sub8 == 0, edge[0], jnp.where(sub8 == 1, edge[1], edge[2]))

    pl.semaphore_wait(barrier, len(peers))
    to_south = remote(sy, ny, 1, 0)
    to_east = remote(sx, wx, 0, 1)
    to_south.start()
    to_east.start()

    for load in loads[3:]:
        load.wait()
    t_east = remote(v0.at[:, TILES - 1, pl.ds(0, ROWS)], rw.at[0], 0, 1)
    t_west = remote(v0.at[:, 0, pl.ds(0, ROWS)], re.at[0], 0, -1)
    t_east.start()
    t_west.start()

    def rhs_body(c, carry):
        before = None
        for t in range(TILES):
            x = picked(gx, c, t, slice(0, ROWS))
            y = picked(gy, c, t, slice(0, ROWS))
            moved = right(x)
            west = jnp.where(first, 0.0 if t == 0 else before, moved)
            before = moved
            north = jnp.where(row16 == 0, 0.0, down(y))
            b0[c, t, 0:ROWS] = screening * v0[c, t, 0:ROWS] - ((x - west) + (y - north))
        return carry

    lax.fori_loop(0, CH, rhs_body, 0)

    to_south.wait()
    to_east.wait()
    has_north = jnp.where(lat > 0, 1.0, 0.0).astype(jnp.float32)
    for c in range(CH):
        b0[c, 0, 0:ROWS] = b0[c, 0, 0:ROWS] + jnp.where(first, right(wx[c]), 0.0)
        for t in range(TILES):
            row = pltpu.roll(ny[t], 8 - c, 0) if c else ny[t]
            b0[c, t, 0:8] = b0[c, t, 0:8] + jnp.where(sub8 == 0, row * has_north, 0.0)

    def pack_body(c, carry):
        for t in range(TILES):
            v, b = v0[c, t, 8:16], b0[c, t, 8:16]
            b = b + jnp.where(sub8 == 4, down(v), 0.0)
            ps[c, t] = jnp.where(north_half, pltpu.roll(b, 4, 0), v)
            v, b = v0[c, t, 0:8], b0[c, t, 0:8]
            b = b + jnp.where(sub8 == 3, up(v), 0.0)
            pn[c, t] = jnp.where(north_half, v, pltpu.roll(b, 4, 0))
        return carry

    lax.fori_loop(0, CH, pack_body, 0)

    e0 = [
        remote(ps, rn.at[:, pl.ds(0, TILES)], 1, 0),
        remote(pn, rs.at[:, pl.ds(0, TILES)], -1, 0),
        remote(ps.at[:, TILES - 1], rn.at[:, TILES + 1], 1, 1),
        remote(ps.at[:, 0], rn.at[:, TILES], 1, -1),
        remote(pn.at[:, TILES - 1], rs.at[:, TILES + 1], -1, 1),
        remote(pn.at[:, 0], rs.at[:, TILES], -1, -1),
        remote(b0.at[:, TILES - 1, pl.ds(0, ROWS)], rw.at[1], 0, 1),
        remote(b0.at[:, 0, pl.ds(0, ROWS)], re.at[1], 0, -1),
    ]
    for copy in e0:
        copy.start()

    inside0, f0 = factors(0, R0, nlat * ROWS, lambda i: jnp.where(i < 20, i, i - 24))
    inside1, f1 = factors(1, R1, nlat * ROWS // 2, lambda i: i - 24)
    inside2, f2 = factors(2, R2, nlat * ROWS // 4, lambda i: i - 8)
    insidep, fp = factors(1, RP, nlat * ROWS // 2, lambda i: i - 8)

    for copy in e0:
        copy.wait()
    t_east.wait()
    t_west.wait()

    in8 = inside0[16:24]

    def halo(south, north):
        v = jnp.where(north_half, south, north) * in8
        b = pltpu.roll(jnp.where(north_half, north, south), 4, 0)
        b = b - jnp.where(sub8 == 3, up(v), jnp.where(sub8 == 4, down(v), 0.0))
        return v, b

    def fill_body(c, carry):
        for t in range(TILES):
            v, b = halo(rs[c, t], rn[c, t])
            v0[c, t, 16:24] = v
            b0[c, t, 16:24] = b
        v, b = halo(
            jnp.where(low8, rs[c, TILES], rs[c, TILES + 1]), jnp.where(low8, rn[c, TILES], rn[c, TILES + 1])
        )
        v0[c, TILES, 16:24] = v
        b0[c, TILES, 16:24] = b
        v0[c, TILES, 0:ROWS] = jnp.where(low, re[0, c], rw[0, c])
        b0[c, TILES, 0:ROWS] = jnp.where(low, re[1, c], rw[1, c])
        return carry

    lax.fori_loop(0, CH, fill_body, 0)

    for i in range(MAXS):
        a, b = (v0, w0) if i % 2 == 0 else (w0, v0)
        sweep(a, b, b0, T0, R0, 0, f0[i], 1.0)

    own = pl.ds(24, 8)
    restrict(v0, b0, b1, 24, tmp, T0, R0, 0, 8, 1.0)
    e1 = [remote(b1.at[:, :, own], b1.at[:, :, pl.ds(24 - 8 * d, 8)], d, 0) for d in (2, -2, 1, -1, 3, -3)]
    e2 = [remote(v0.at[:, :, pl.ds(0, 8)], zs, -1, 0), remote(v0.at[:, :, pl.ds(8, 8)], zn, 1, 0)]
    for copy in e1 + e2:
        copy.start()
    for copy in e1:
        copy.wait()

    def first1(c, carry):
        for t in range(T1):
            v1[c, t] = f1[0] * b1[c, t]
        return carry

    lax.fori_loop(0, CH, first1, 0)
    sweep(v1, w1, b1, T1, R1, 0, f1[1], 0.25)
    sweep(w1, v1, b1, T1, R1, 0, f1[2], 0.25)
    sweep(v1, w1, b1, T1, R1, 0, f1[3], 0.25)
    restrict(w1, b1, b2, 0, tmp, T1, R1, 8, R2, 0.25)

    def first2(c, carry):
        for t in range(T2):
            v2[c, t] = f2[0] * b2[c, t]
        return carry

    lax.fori_loop(0, CH, first2, 0)
    sweep(v2, w2, b2, T2, R2, 0, f2[1], 0.0625)
    sweep(w2, v2, b2, T2, R2, 0, f2[2], 0.0625)
    sweep(v2, w2, b2, T2, R2, 0, f2[3], 0.0625)

    def up1(c, carry):
        prolong_rows(w2, c, T2, R2, tmp)
        fine = prolong_cols([tmp[t, 8:32] for t in range(T2)], RP)
        for t in range(T1):
            vp[c, t] = (w1[c, t, 16:40] + fine[t]) * insidep
        return carry

    lax.fori_loop(0, CH, up1, 0)
    for i in range(MAXS):
        a, b = (vp, wp) if i % 2 == 0 else (wp, vp)
        sweep(a, b, b1, T1, RP, 16, fp[i], 0.25)

    for copy in e2:
        copy.wait()

    def up0(c, carry):
        prolong_rows(vp, c, T1, RP, tmp)
        ends = [jnp.where(north_half, tmp[t, 32:40], tmp[t, 8:16]) for t in range(T1)]
        mids = prolong_cols([tmp[t, 16:32] for t in range(T1)], ROWS)
        ends = prolong_cols(ends, 8)
        for t in range(T0):
            v0[c, t, 0:ROWS] = v0[c, t, 0:ROWS] + mids[t]
            v0[c, t, 16:24] = (jnp.where(north_half, zs[c, t], zn[c, t]) + ends[t]) * in8
        return carry

    lax.fori_loop(0, CH, up0, 0)
    for i in range(MAXS):
        a, b = (v0, w0) if i % 2 == 0 else (w0, v0)
        sweep(a, b, b0, T0, R0, 0, f0[i], 1.0)
    for c in range(CH):
        for t in range(TILES):
            out[c, :, t * L : (t + 1) * L] = v0[c, t, 0:ROWS]


def local(target, grad_x, grad_y, labels, sweeps):
    f32 = jnp.float32

    def vmem(*shape):
        return pltpu.VMEM(shape + (L,), f32)

    scratch = [
        pltpu.VMEM(grad_x.shape, f32),
        pltpu.VMEM(grad_y.shape, f32),
        pltpu.VMEM(labels.shape, jnp.int32),
        vmem(CH, T0, R0), vmem(CH, T0, R0), vmem(CH, T0, R0),
        vmem(CH, ROWS), vmem(CH, ROWS),
        vmem(TILES, 8), vmem(TILES, 8),
        vmem(CH, TILES, 8), vmem(CH, TILES, 8),
        vmem(CH, TILES + 2, 8), vmem(CH, TILES + 2, 8),
        vmem(2, CH, ROWS), vmem(2, CH, ROWS),
        vmem(CH, T1, R1), vmem(CH, T1, R1), vmem(CH, T1, R1),
        vmem(CH, T1, RP), vmem(CH, T1, RP),
        vmem(CH, T2, R2), vmem(CH, T2, R2), vmem(CH, T2, R2),
        vmem(CH, T0, 8), vmem(CH, T0, 8),
        vmem(T0, R1),
        pltpu.SemaphoreType.DMA((3 + TILES,)),
        pltpu.SemaphoreType.DMA((20,)),
        pltpu.SemaphoreType.DMA((20,)),
    ]
    anywhere = pl.BlockSpec(memory_space=pl.ANY)
    return pl.pallas_call(
        kernel,
        out_shape=jax.ShapeDtypeStruct(target.shape, f32),
        in_specs=[pl.BlockSpec(memory_space=pltpu.SMEM)] + [anywhere] * 4,
        out_specs=pl.BlockSpec(memory_space=pltpu.VMEM),
        scratch_shapes=scratch,
        compiler_params=pltpu.CompilerParams(collective_id=0, has_side_effects=True),
        name="vcycle",
    )(sweeps, target, grad_x, grad_y, labels)


def solution(mesh):
    in_specs = (
        P(None, "lat", "lon"),
        P(None, None, "lat", "lon"),
        P(None, None, "lat", "lon"),
        P("lat", "lon"),
        P(),
    )
    out_specs = P(None, "lat", "lon")
    return jax.shard_map(local, mesh=mesh, in_specs=in_specs, out_specs=out_specs, check_vma=False)
```

time: 286 us -> 44.7 us (0.16); the launches traced: 282 us -> 44.5 us
  starting transfers between devices: 147 us -> 0 us
  waiting for transfers between devices: 61.1 us -> 0 us
  Pallas kernels: 0 us -> 42.9 us
  local copies, waits for them, and re-layouts: 43.2 us -> 1.62 us
  other arithmetic: 18.7 us -> 0 us
  loops' own time: 11.6 us -> 0 us
    ppermute x38 -> x0, starting transfers between devices: 147 us -> none  [the longest x18 105 us: with_halo(): lax.ppermute(head, axis, [((i + 1) % count, i) for i in range(ends)])]
    ppermute x38 -> x0, waiting for transfers between devices: 61.1 us -> none  [the longest x18 48.1 us: with_halo(): lax.ppermute(head, axis, [((i + 1) % count, i) for i in range(ends)])]
    pallas_call x0 -> x1, Pallas kernels: none -> 42.9 us  [local(): pl.pallas_call(kernel, out_shape=jax.ShapeDtypeStruct(target.shape, f32),...]
    reshape x4 -> x0, local copies, waits for them, and re-layouts: 30.5 us -> none  [the longest x2 17.9 us: restrict(): return field.reshape(chans, rows // 2, 2, cols // 2, 2).mean(axis=(2, 4))]
    another operation x5 -> x0, loops' own time: 11.6 us -> none  [smooth(): value = lax.fori_loop(0, count, sweep_wide, value)]
    another operation x2 -> x0, local copies, waits for them, and re-layouts: 8.5 us -> none  [prolong_from(): jnp.stack([jnp.stack([f00, f01], -1), jnp.stack([f10, f11], -1)], 2)]
    reduce_sum x2 -> x0, other arithmetic: 6.77 us -> none  [restrict(): return field.reshape(chans, rows // 2, 2, cols // 2, 2).mean(axis=(2, 4))]
    slice x24 -> x0, local copies, waits for them, and re-layouts: 3.41 us -> none  [the longest x1 1.43 us: cycle(): count = sweeps[level]]
  transfers between devices with their start and end apart: 38 -> 0, of which waited for: 22 -> 0; matrix products, arithmetic and copies ran while one was open for 1% -> 0% of each run, Pallas kernels for 0% -> 0%
where the time goes in v1:
time: 44.7 us; the launch traced here: 44.5 us
  Pallas kernels  42.9 us (96%)
  local copies, waits for them, and re-layouts  1.62 us (4%)
    pallas_call x1, Pallas kernels, local(): pl.pallas_call(kernel, out_shape=jax.ShapeDtypeStruct(target.shape, f32),...  42.9 us
    unnamed x1, local copies, waits for them, and re-layouts  1.62 us

profile of v1, /device:TPU:6, one launch (start us, length us, event | category | flops | bytes accessed | tf_op | source)
XLA Modules:
  0.0 44.5 jit_solution(16746321073903944283)
XLA Ops:
  0.0 42.9 %vcycle.1 = f32[3,16,1024]{2,1,0:T(8,128)} custom-call(s32[3]{0:T(128)} %sweeps.1, f32[3,16,1024]{2,1,0:T(8,128)} %target.1, f32[2,3,16,1024]{3,2,1,0:T(8,128)} %grad_x.1, f32[2,3,16,1024]{3,2,1,0:T(8,128)} %grad_y.1, s32[16,1024]{1,0:T(8,128)} %labels.1), custom_call_target="tpu_custom_call" | custom-call | tf_op jit(solution)/shard_map/vcycle/pallas_call | solution.py:397
  42.9 1.6 %copy.7 = f32[3,16,1024]{2,1,0:T(8,128)} copy(f32[3,16,1024]{2,1,0:T(8,128)} %vcycle.1) | data formatting | bytes 393216

commit v2 on v1

v2 whole, which is shorter than its diff:
```python
import jax
import jax.numpy as jnp
from jax import lax
from jax.experimental import pallas as pl
from jax.experimental.pallas import tpu as pltpu
from jax.sharding import PartitionSpec as P

SOURCES = 2
LEVELS = 3
MAXS = 4
CH = 3
ROWS = 16
TILES = 8
L = 128

screening = 0.02
damping = 0.8
MESH = pl.DeviceIdType.MESH

T0, T1, T2 = TILES + 1, TILES // 2 + 1, TILES // 4 + 1
O0, R0 = 8, 32
O1, R1 = 24, 56
OP, RP = 8, 32
O2, R2 = 8, 24


def iota(rows, dim):
    return lax.broadcasted_iota(jnp.int32, (rows, L), dim)


def lanes_of(rows):
    lane = iota(rows, 1)
    return lane == 0, lane == L - 1, lane < L // 2


def rolled(x, shift, dim):
    shift %= x.shape[dim]
    return pltpu.roll(x, shift, dim) if shift else x


def residual(src, rhs, c, t, tiles, at, rhs_at, rows, scale):
    diag = screening + 4.0 * scale
    first, last, _ = lanes_of(rows)
    x = src[c, t, at : at + rows]
    before = src[c, (t - 1) % tiles, at : at + rows]
    after = src[c, (t + 1) % tiles, at : at + rows]
    west = rolled(jnp.where(last, before, x), 1, 1)
    east = rolled(jnp.where(first, after, x), -1, 1)
    north = src[c, t, at - 1 : at - 1 + rows]
    south = src[c, t, at + 1 : at + 1 + rows]
    beside = (north + south) + (west + east)
    if scale != 1.0:
        beside = scale * beside
    return x, (rhs[c, t, rhs_at : rhs_at + rows] - diag * x) + beside


def sweep(src, dst, rhs, tiles, at, rhs_at, rows, factor, scale):
    for c in range(CH):
        for t in range(tiles):
            x, r = residual(src, rhs, c, t, tiles, at, rhs_at, rows, scale)
            dst[c, t, at : at + rows] = x + factor * r


def restrict(src, rhs, dst, tmp, tiles, at, rhs_at, rows, dst_at, count, scale):
    low = lanes_of(count)[2]
    pick = (2 * iota(count, 1)) % L
    for c in range(CH):
        for t in range(tiles):
            tmp[c, t, 0:rows] = residual(src, rhs, c, t, tiles, at, rhs_at, rows, scale)[1]
        parts = []
        for t in range(tiles):
            pair = tmp[c, t, pl.ds(0, count, stride=2)] + tmp[c, t, pl.ds(1, count, stride=2)]
            pair = pair + rolled(pair, -1, 1)
            parts.append(0.25 * jnp.take_along_axis(pair, pick, axis=1))
        for t in range(tiles // 2):
            dst[c, t, dst_at : dst_at + count] = jnp.where(low, parts[2 * t], parts[2 * t + 1])
        dst[c, tiles // 2, dst_at : dst_at + count] = parts[-1]


def prolong_rows(src, c, tiles, at, rows, tmp):
    for t in range(tiles):
        x = 0.75 * src[c, t, at : at + rows]
        tmp[c, t, pl.ds(0, rows, stride=2)] = x + 0.25 * src[c, t, at - 1 : at - 1 + rows]
        tmp[c, t, pl.ds(1, rows, stride=2)] = x + 0.25 * src[c, t, at + 1 : at + 1 + rows]


def prolong_cols(xs, rows):
    lane = iota(rows, 1)
    first, last, low = lanes_of(rows)
    aside = jnp.where(lane % 2 == 0, L - 1, 1)
    count = len(xs)
    out = []
    for t in range(count):
        wests = rolled(xs[t - 1], 1, 1)
        easts = rolled(xs[(t + 1) % count], -1, 1)
        for h in range(2 if t < count - 1 else 1):
            here = lane // 2 + (h * (L // 2) if t < count - 1 else jnp.where(low, 0, L // 2))
            near = jnp.take_along_axis(xs[t], here, axis=1)
            far = jnp.take_along_axis(xs[t], (here + aside) % L, axis=1)
            if h == 0:
                far = jnp.where(first, wests, far)
            if h == 1 or t == count - 1:
                far = jnp.where(last, easts, far)
            out.append(0.75 * near + 0.25 * far)
    return out


def kernel(
    sweeps, target, grad_x, grad_y, labels, out,
    gx, gy, lab, v0, w0, b0, sy, sx, ny, ey, wy, wx, xn, xs, xnw, xsw,
    ps, pn, rn, rs, pe, pw, re, rw,
    b1, v1, w1, vp, wp, b2, v2, w2, zn, zs, fn, fs, gn, gs, tmp,
    in_sem, send, recv,
):
    lon, lat = lax.axis_index("lon"), lax.axis_index("lat")
    nlon, nlat = lax.axis_size("lon"), lax.axis_size("lat")

    def peer(dlat, dlon):
        return {"lat": lax.rem(lat + dlat + nlat, nlat), "lon": lax.rem(lon + dlon + nlon, nlon)}

    peers = [(d, 0) for d in (1, -1, 2, -2, 3, -3)]
    peers += [(i, j) for i in (-1, 0, 1) for j in (-1, 1)]
    barrier = pltpu.get_barrier_semaphore()
    for dlat, dlon in peers:
        pl.semaphore_signal(barrier, inc=1, device_id=peer(dlat, dlon), device_id_type=MESH)

    loads = [
        pltpu.make_async_copy(labels, lab, in_sem.at[0]),
        pltpu.make_async_copy(grad_x, gx, in_sem.at[1]),
        pltpu.make_async_copy(grad_y, gy, in_sem.at[2]),
    ]
    for t in range(TILES):
        loads.append(
            pltpu.make_async_copy(
                target.at[:, :, pl.ds(t * L, L)], v0.at[:, t, pl.ds(O0, ROWS)], in_sem.at[3 + t]
            )
        )
    for load in loads:
        load.start()

    used = [0]

    def remote(src, dst, dlat, dlon):
        k = used[0]
        used[0] += 1
        return pltpu.make_async_remote_copy(
            src_ref=src,
            dst_ref=dst,
            send_sem=send.at[k],
            recv_sem=recv.at[k],
            device_id=peer(dlat, dlon),
            device_id_type=MESH,
        )

    first, last, low = lanes_of(ROWS)
    first8, last8, low8 = lanes_of(8)
    sub = iota(8, 0)
    lane = iota(ROWS, 1)
    upper = sub < 4
    row = iota(ROWS, 0)

    def inside(level, start, rows):
        here = iota(rows, 0) + (start + lat * (ROWS >> level))
        return jnp.where((here >= 0) & (here < (nlat * ROWS >> level)), 1.0, 0.0).astype(jnp.float32)

    def step(level, i):
        full = damping / (screening + 4.0 * 0.25**level)
        return jnp.where(sweeps[level] > i, full, 0.0).astype(jnp.float32)

    for c in range(CH):
        for t in range(T0):
            for ref in (v0, w0):
                ref[c, t, 0:8] = jnp.zeros((8, L), jnp.float32)
                ref[c, t, 24:32] = jnp.zeros((8, L), jnp.float32)

    for load in loads[:3]:
        load.wait()

    def picked(ref, c, t, rows):
        cols = slice(t * L, (t + 1) * L)
        return jnp.where(lab[rows, cols] == 0, ref[0, c, rows, cols], ref[1, c, rows, cols])

    for t in range(TILES):
        edge = [rolled(picked(gy, c, t, slice(8, 16)), c + 1, 0) for c in range(CH)]
        sy[t] = jnp.where(sub == 0, edge[0], jnp.where(sub == 1, edge[1], edge[2]))
    edge = [rolled(picked(gx, c, TILES - 1, slice(0, ROWS)), c + 1, 1) for c in range(CH)]
    sx[...] = jnp.where(lane == 0, edge[0], jnp.where(lane == 1, edge[1], edge[2]))

    pl.semaphore_wait(barrier, len(peers))
    north8, south8 = pl.ds(0, 8), pl.ds(8, 8)
    edges = [
        remote(sy, ny.at[pl.ds(0, TILES)], 1, 0),
        remote(sy.at[0], ny.at[TILES], 1, -1),
        remote(sy.at[TILES - 1], ny.at[TILES + 1], 1, 1),
        remote(sy.at[0], ey, 0, -1),
        remote(sy.at[TILES - 1], wy, 0, 1),
        remote(sx, wx, 0, 1),
        remote(sx.at[north8], xs, -1, 0),
        remote(sx.at[south8], xn, 1, 0),
        remote(sx.at[north8], xsw, -1, 1),
        remote(sx.at[south8], xnw, 1, 1),
    ]
    for copy in edges:
        copy.start()
    for load in loads[3:]:
        load.wait()

    own = slice(O0, O0 + ROWS)
    for c in range(CH):
        before = None
        for t in range(TILES):
            x = picked(gx, c, t, slice(0, ROWS))
            y = picked(gy, c, t, slice(0, ROWS))
            moved = rolled(x, 1, 1)
            west = jnp.where(first, 0.0 if t == 0 else before, moved)
            before = moved
            north = jnp.where(row == 0, 0.0, rolled(y, 1, 0))
            v = v0[c, t, own]
            b = screening * v - ((x - west) + (y - north))
            b0[c, t, own] = b
            vn, vs, bn, bs = v[0:8], v[8:16], b[0:8], b[8:16]
            bs = bs + jnp.where(sub == 4, rolled(vs, 1, 0), 0.0)
            ps[c, t] = jnp.where(upper, rolled(bs, 4, 0), vs)
            bn = bn + jnp.where(sub == 3, rolled(vn, -1, 0), 0.0)
            pn[c, t] = jnp.where(upper, vn, rolled(bn, 4, 0))
            if t == 0:
                pw[c] = jnp.where(low, v, rolled(b, L // 2, 1))
            if t == TILES - 1:
                pe[c] = jnp.where(low, rolled(b, L // 2, 1), v)

    e0 = [
        remote(ps, rn.at[:, pl.ds(0, TILES)], 1, 0),
        remote(pn, rs.at[:, pl.ds(0, TILES)], -1, 0),
        remote(pe, rw, 0, 1),
        remote(pw, re, 0, -1),
        remote(ps.at[:, TILES - 1], rn.at[:, TILES + 1], 1, 1),
        remote(ps.at[:, 0], rn.at[:, TILES], 1, -1),
        remote(pn.at[:, TILES - 1], rs.at[:, TILES + 1], -1, 1),
        remote(pn.at[:, 0], rs.at[:, TILES], -1, -1),
    ]
    for copy in e0:
        copy.start()

    inside0 = inside(0, -8, R0)
    has_north = jnp.where(lat > 0, 1.0, 0.0).astype(jnp.float32)
    for copy in edges:
        copy.wait()

    def column(x, c):
        return jnp.where(first if x.shape[0] == ROWS else first8, rolled(x, -c, 1), 0.0)

    def line(x, c):
        return jnp.where(sub == 0, rolled(x, -c, 0), 0.0)

    for c in range(CH):
        b0[c, 0, own] = b0[c, 0, own] + column(wx[...], c)
        for t in range(TILES):
            b0[c, t, 8:16] = b0[c, t, 8:16] + has_north * line(ny[t], c)

    for copy in e0:
        copy.wait()

    for c in range(CH):
        halves = [(rn[c, t], rs[c, t]) for t in range(TILES)]
        halves.append(
            (jnp.where(low8, rn[c, TILES], rn[c, TILES + 1]), jnp.where(low8, rs[c, TILES], rs[c, TILES + 1]))
        )
        for t, (n, s) in enumerate(halves):
            v0[c, t, 0:8] = jnp.where(upper, 0.0, n) * inside0[0:8]
            v0[c, t, 24:32] = jnp.where(upper, s, 0.0) * inside0[24:32]
            n, s = rolled(n, 4, 0), rolled(s, 4, 0)
            below = sy[t] if t < TILES else jnp.where(low8, ey[...], wy[...])
            s = s + line(below, c)
            if t == 0:
                n, s = n + column(xnw[...], c), s + column(xsw[...], c)
            if t == TILES:
                n, s = n + column(xn[...], c), s + column(xs[...], c)
            b0[c, t, 0:8] = n
            b0[c, t, 24:32] = s
        v0[c, TILES, own] = jnp.where(low, re[c], rw[c])
        b = rolled(jnp.where(low, rw[c], re[c]), L // 2, 1) + column(sx[...], c)
        above = has_north * line(jnp.where(low8, ny[TILES], ny[TILES + 1]), c)
        b0[c, TILES, 8:16] = b[0:8] + above
        b0[c, TILES, 16:24] = b[8:16]

    for i in range(MAXS):
        a, b = (v0, w0) if i % 2 == 0 else (w0, v0)
        sweep(a, b, b0, T0, 4, 4, 24, inside0[4:28] * step(0, i), 1.0)

    restrict(v0, b0, b1, tmp, T0, O0, O0, ROWS, O1, 8, 1.0)
    for t in range(T1):
        rows = [b1[c, t, O1 : O1 + 8] for c in range(CH)]
        n, s = ([rolled(x, 2 * c + k, 0) for c, x in enumerate(rows)] for k in (0, 2))
        fn[t] = jnp.where(sub < 2, n[0], jnp.where(upper, n[1], n[2]))
        fs[t] = jnp.where(sub < 2, s[0], jnp.where(upper, s[1], s[2]))
    mine = b1.at[:, :, pl.ds(O1, 8)]
    e1 = [remote(mine, b1.at[:, :, pl.ds(O1 - 8 * d, 8)], d, 0) for d in (2, -2)]
    e1 += [remote(fs, gn, 3, 0), remote(fn, gs, -3, 0)]
    e1 += [remote(mine, b1.at[:, :, pl.ds(O1 - 8 * d, 8)], d, 0) for d in (1, -1)]
    e2 = [
        remote(v0.at[:, :, pl.ds(O0, 8)], zs, -1, 0),
        remote(v0.at[:, :, pl.ds(O0 + 8, 8)], zn, 1, 0),
    ]
    for copy in e1 + e2:
        copy.start()

    def factor(level, i, base, at, rows):
        return inside(level, at - base, rows) * step(level, i)

    for copy in e1:
        copy.wait()
    for c in range(CH):
        for t in range(T1):
            b1[c, t, 0:8] = rolled(gn[t], -2 * c - 2, 0)
            b1[c, t, 48:56] = rolled(gs[t], -2 * c, 0)

    f = factor(1, 0, O1, 0, R1)
    for c in range(CH):
        for t in range(T1):
            v1[c, t] = f * b1[c, t]
    sweep(v1, w1, b1, T1, 4, 4, 48, factor(1, 1, O1, 4, 48), 0.25)
    sweep(w1, v1, b1, T1, 8, 8, 40, factor(1, 2, O1, 8, 40), 0.25)
    sweep(v1, w1, b1, T1, 8, 8, 40, factor(1, 3, O1, 8, 40), 0.25)
    for c in range(CH):
        for t in range(T1):
            tmp[c, t, 40:48] = jnp.zeros((8, L), jnp.float32)
    restrict(w1, b1, b2, tmp, T1, 8, 8, 40, 0, R2, 0.25)

    f = factor(2, 0, O2, 0, R2)
    for c in range(CH):
        for t in range(T2):
            v2[c, t] = f * b2[c, t]
    for i in range(1, MAXS):
        a, b = (v2, w2) if i % 2 else (w2, v2)
        sweep(a, b, b2, T2, 2, 2, 16, factor(2, i, O2, 2, 16), 0.0625)

    insidep = inside(1, -OP, 24)
    for c in range(CH):
        prolong_rows(w2, c, T2, 4, 16, tmp)
        fine = prolong_cols([tmp[c, t, 0:24] for t in range(T2)], 24)
        for t in range(T1):
            vp[c, t, 0:24] = (w1[c, t, 16:40] + fine[t]) * insidep
    for i, (at, rows) in enumerate(((1, 24), (1, 24), (4, 16), (4, 16))):
        a, b = (vp, wp) if i % 2 == 0 else (wp, vp)
        sweep(a, b, b1, T1, at, at + O1 - OP, rows, factor(1, i, OP, at, rows), 0.25)

    for copy in e2:
        copy.wait()
    for c in range(CH):
        prolong_rows(vp, c, T1, 4, 16, tmp)
        fine = prolong_cols([tmp[c, t, 0:32] for t in range(T1)], 32)
        for t in range(T0):
            v0[c, t, 0:8] = (zn[c, t] + fine[t][0:8]) * inside0[0:8]
            v0[c, t, own] = v0[c, t, own] + fine[t][8:24]
            v0[c, t, 24:32] = (zs[c, t] + fine[t][24:32]) * inside0[24:32]
    for i in range(MAXS - 1):
        a, b = (v0, w0) if i % 2 == 0 else (w0, v0)
        sweep(a, b, b0, T0, 4, 4, 24, inside0[4:28] * step(0, i), 1.0)
    f = step(0, MAXS - 1)
    for c in range(CH):
        for t in range(TILES):
            x, r = residual(w0, b0, c, t, T0, O0, O0, ROWS, 1.0)
            out[c, :, t * L : (t + 1) * L] = x + f * r


def local(target, grad_x, grad_y, labels, sweeps):
    f32 = jnp.float32

    def vmem(*shape):
        return pltpu.VMEM(shape + (L,), f32)

    scratch = [
        pltpu.VMEM(grad_x.shape, f32),
        pltpu.VMEM(grad_y.shape, f32),
        pltpu.VMEM(labels.shape, jnp.int32),
        vmem(CH, T0, R0), vmem(CH, T0, R0), vmem(CH, T0, R0),
        vmem(TILES, 8), vmem(ROWS),
        vmem(TILES + 2, 8), vmem(8), vmem(8), vmem(ROWS),
        vmem(8), vmem(8), vmem(8), vmem(8),
        vmem(CH, TILES, 8), vmem(CH, TILES, 8),
        vmem(CH, TILES + 2, 8), vmem(CH, TILES + 2, 8),
        vmem(CH, ROWS), vmem(CH, ROWS), vmem(CH, ROWS), vmem(CH, ROWS),
        vmem(CH, T1, R1), vmem(CH, T1, R1), vmem(CH, T1, R1),
        vmem(CH, T1, RP), vmem(CH, T1, RP),
        vmem(CH, T2, R2), vmem(CH, T2, R2), vmem(CH, T2, R2),
        vmem(CH, T0, 8), vmem(CH, T0, 8),
        vmem(T1, 8), vmem(T1, 8), vmem(T1, 8), vmem(T1, 8),
        vmem(CH, T0, 48),
        pltpu.SemaphoreType.DMA((3 + TILES,)),
        pltpu.SemaphoreType.DMA((26,)),
        pltpu.SemaphoreType.DMA((26,)),
    ]
    anywhere = pl.BlockSpec(memory_space=pl.ANY)
    return pl.pallas_call(
        kernel,
        out_shape=jax.ShapeDtypeStruct(target.shape, f32),
        in_specs=[pl.BlockSpec(memory_space=pltpu.SMEM)] + [anywhere] * 4,
        out_specs=pl.BlockSpec(memory_space=pltpu.VMEM),
        scratch_shapes=scratch,
        compiler_params=pltpu.CompilerParams(collective_id=0, has_side_effects=True),
        name="vcycle",
    )(sweeps, target, grad_x, grad_y, labels)


def solution(mesh):
    in_specs = (
        P(None, "lat", "lon"),
        P(None, None, "lat", "lon"),
        P(None, None, "lat", "lon"),
        P("lat", "lon"),
        P(),
    )
    out_specs = P(None, "lat", "lon")
    return jax.shard_map(local, mesh=mesh, in_specs=in_specs, out_specs=out_specs, check_vma=False)
```

time: 44.7 us -> 36.4 us (0.81)
  Pallas kernels: 42.9 us -> 34.4 us
    pallas_call x1, Pallas kernels: 42.9 us -> 34.4 us  [local(): pl.pallas_call(kernel, out_shape=jax.ShapeDtypeStruct(target.shape, f32),...]
where the time goes in v2:
time: 36.4 us; the launch traced here: 36.1 us
  Pallas kernels  34.4 us (95%)
  local copies, waits for them, and re-layouts  1.62 us (4%)
    pallas_call x1, Pallas kernels, local(): pl.pallas_call(kernel, out_shape=jax.ShapeDtypeStruct(target.shape, f32),...  34.4 us
    unnamed x1, local copies, waits for them, and re-layouts  1.62 us

profile of v2, /device:TPU:6, one launch (start us, length us, event | category | flops | bytes accessed | tf_op | source)
XLA Modules:
  0.0 36.1 jit_solution(15523827445571530011)
XLA Ops:
  0.0 34.4 %vcycle.1 = f32[3,16,1024]{2,1,0:T(8,128)} custom-call(s32[3]{0:T(128)} %sweeps.1, f32[3,16,1024]{2,1,0:T(8,128)} %target.1, f32[2,3,16,1024]{3,2,1,0:T(8,128)} %grad_x.1, f32[2,3,16,1024]{3,2,1,0:T(8,128)} %grad_y.1, s32[16,1024]{1,0:T(8,128)} %labels.1), custom_call_target="tpu_custom_call" | custom-call | tf_op jit(solution)/shard_map/vcycle/pallas_call | solution.py:394
  34.4 1.6 %copy.7 = f32[3,16,1024]{2,1,0:T(8,128)} copy(f32[3,16,1024]{2,1,0:T(8,128)} %vcycle.1) | data formatting | bytes 393216

commit v3 on v2

--- a/solution.py
+++ b/solution.py
@@ -22,6 +22,7 @@
 O1, R1 = 24, 56
 OP, RP = 8, 32
 O2, R2 = 8, 24
+WIDE = 21
 
 
 def iota(rows, dim):
@@ -109,7 +110,7 @@
     sweeps, target, grad_x, grad_y, labels, out,
     gx, gy, lab, v0, w0, b0, sy, sx, ny, ey, wy, wx, xn, xs, xnw, xsw,
     ps, pn, rn, rs, pe, pw, re, rw,
-    b1, v1, w1, vp, wp, b2, v2, w2, zn, zs, fn, fs, gn, gs, tmp,
+    b1, v1, w1, vp, wp, b2, v2, w2, zn, zs, un, us, hs, fn, fs, gn, gs, tmp,
     in_sem, send, recv,
 ):
     lon, lat = lax.axis_index("lon"), lax.axis_index("lat")
@@ -154,8 +155,9 @@
 
     first, last, low = lanes_of(ROWS)
     first8, last8, low8 = lanes_of(8)
+    low4 = lanes_of(4)[2]
     sub = iota(8, 0)
-    lane = iota(ROWS, 1)
+    lane, lane8 = iota(ROWS, 1), iota(8, 1)
     upper = sub < 4
     row = iota(ROWS, 0)
 
@@ -182,7 +184,7 @@
 
     for t in range(TILES):
         edge = [rolled(picked(gy, c, t, slice(8, 16)), c + 1, 0) for c in range(CH)]
-        sy[t] = jnp.where(sub == 0, edge[0], jnp.where(sub == 1, edge[1], edge[2]))
+        sy[t] = jnp.where(sub == 0, edge[0], jnp.where(sub == 1, edge[1], edge[2]))[0:4]
     edge = [rolled(picked(gx, c, TILES - 1, slice(0, ROWS)), c + 1, 1) for c in range(CH)]
     sx[...] = jnp.where(lane == 0, edge[0], jnp.where(lane == 1, edge[1], edge[2]))
 
@@ -250,7 +252,7 @@
         return jnp.where(first if x.shape[0] == ROWS else first8, rolled(x, -c, 1), 0.0)
 
     def line(x, c):
-        return jnp.where(sub == 0, rolled(x, -c, 0), 0.0)
+        return jnp.where(sub == 0, x[c : c + 1], 0.0)
 
     for c in range(CH):
         b0[c, 0, own] = b0[c, 0, own] + column(wx[...], c)
@@ -269,7 +271,7 @@
             v0[c, t, 0:8] = jnp.where(upper, 0.0, n) * inside0[0:8]
             v0[c, t, 24:32] = jnp.where(upper, s, 0.0) * inside0[24:32]
             n, s = rolled(n, 4, 0), rolled(s, 4, 0)
-            below = sy[t] if t < TILES else jnp.where(low8, ey[...], wy[...])
+            below = sy[t] if t < TILES else jnp.where(low4, ey[...], wy[...])
             s = s + line(below, c)
             if t == 0:
                 n, s = n + column(xnw[...], c), s + column(xsw[...], c)
@@ -279,7 +281,7 @@
             b0[c, t, 24:32] = s
         v0[c, TILES, own] = jnp.where(low, re[c], rw[c])
         b = rolled(jnp.where(low, rw[c], re[c]), L // 2, 1) + column(sx[...], c)
-        above = has_north * line(jnp.where(low8, ny[TILES], ny[TILES + 1]), c)
+        above = has_north * line(jnp.where(low4, ny[TILES], ny[TILES + 1]), c)
         b0[c, TILES, 8:16] = b[0:8] + above
         b0[c, TILES, 16:24] = b[8:16]
 
@@ -293,15 +295,30 @@
         n, s = ([rolled(x, 2 * c + k, 0) for c, x in enumerate(rows)] for k in (0, 2))
         fn[t] = jnp.where(sub < 2, n[0], jnp.where(upper, n[1], n[2]))
         fs[t] = jnp.where(sub < 2, s[0], jnp.where(upper, s[1], s[2]))
-    mine = b1.at[:, :, pl.ds(O1, 8)]
-    e1 = [remote(mine, b1.at[:, :, pl.ds(O1 - 8 * d, 8)], d, 0) for d in (2, -2)]
+    turned = [rolled(b1[c, T1 - 1, O1 : O1 + 8], WIDE + 2 * WIDE * c, 1) for c in range(CH)]
+    hs[O1 : O1 + 8] = jnp.where(lane8 < 2 * WIDE, turned[0], jnp.where(lane8 < 4 * WIDE, turned[1], turned[2]))
+
+    def sent(d):
+        rows, there = pl.ds(O1, 8), pl.ds(O1 - 8 * d, 8)
+        return [
+            remote(b1.at[:, pl.ds(0, T1 - 1), rows], b1.at[:, pl.ds(0, T1 - 1), there], d, 0),
+            remote(hs.at[rows], hs.at[there], d, 0),
+        ]
+
+    e1 = sent(2) + sent(-2)
     e1 += [remote(fs, gn, 3, 0), remote(fn, gs, -3, 0)]
-    e1 += [remote(mine, b1.at[:, :, pl.ds(O1 - 8 * d, 8)], d, 0) for d in (1, -1)]
+    e1 += sent(1) + sent(-1)
     e2 = [
-        remote(v0.at[:, :, pl.ds(O0, 8)], zs, -1, 0),
-        remote(v0.at[:, :, pl.ds(O0 + 8, 8)], zn, 1, 0),
+        remote(un, zs, -1, 0),
+        remote(us, zn, 1, 0),
     ]
-    for copy in e1 + e2:
+    for copy in e1:
+        copy.start()
+    for c in range(CH):
+        for t in range(T0):
+            un[c, t] = v0[c, t, O0 : O0 + 4]
+            us[c, t] = v0[c, t, O0 + ROWS - 4 : O0 + ROWS]
+    for copy in e2:
         copy.start()
 
     def factor(level, i, base, at, rows):
@@ -313,6 +330,8 @@
         for t in range(T1):
             b1[c, t, 0:8] = rolled(gn[t], -2 * c - 2, 0)
             b1[c, t, 48:56] = rolled(gs[t], -2 * c, 0)
+        for at, rows in ((8, 16), (32, 16)):
+            b1[c, T1 - 1, at : at + rows] = rolled(hs[at : at + rows], -WIDE - 2 * WIDE * c, 1)
 
     f = factor(1, 0, O1, 0, R1)
     for c in range(CH):
@@ -350,9 +369,9 @@
         prolong_rows(vp, c, T1, 4, 16, tmp)
         fine = prolong_cols([tmp[c, t, 0:32] for t in range(T1)], 32)
         for t in range(T0):
-            v0[c, t, 0:8] = (zn[c, t] + fine[t][0:8]) * inside0[0:8]
+            v0[c, t, 4:8] = (zn[c, t] + fine[t][4:8]) * inside0[4:8]
             v0[c, t, own] = v0[c, t, own] + fine[t][8:24]
-            v0[c, t, 24:32] = (zs[c, t] + fine[t][24:32]) * inside0[24:32]
+            v0[c, t, 24:28] = (zs[c, t] + fine[t][24:28]) * inside0[24:28]
     for i in range(MAXS - 1):
         a, b = (v0, w0) if i % 2 == 0 else (w0, v0)
         sweep(a, b, b0, T0, 4, 4, 24, inside0[4:28] * step(0, i), 1.0)
@@ -374,8 +393,8 @@
         pltpu.VMEM(grad_y.shape, f32),
         pltpu.VMEM(labels.shape, jnp.int32),
         vmem(CH, T0, R0), vmem(CH, T0, R0), vmem(CH, T0, R0),
-        vmem(TILES, 8), vmem(ROWS),
-        vmem(TILES + 2, 8), vmem(8), vmem(8), vmem(ROWS),
+        vmem(TILES, 4), vmem(ROWS),
+        vmem(TILES + 2, 4), vmem(4), vmem(4), vmem(ROWS),
         vmem(8), vmem(8), vmem(8), vmem(8),
         vmem(CH, TILES, 8), vmem(CH, TILES, 8),
         vmem(CH, TILES + 2, 8), vmem(CH, TILES + 2, 8),
@@ -383,12 +402,13 @@
         vmem(CH, T1, R1), vmem(CH, T1, R1), vmem(CH, T1, R1),
         vmem(CH, T1, RP), vmem(CH, T1, RP),
         vmem(CH, T2, R2), vmem(CH, T2, R2), vmem(CH, T2, R2),
-        vmem(CH, T0, 8), vmem(CH, T0, 8),
+        vmem(CH, T0, 4), vmem(CH, T0, 4), vmem(CH, T0, 4), vmem(CH, T0, 4),
+        vmem(R1),
         vmem(T1, 8), vmem(T1, 8), vmem(T1, 8), vmem(T1, 8),
         vmem(CH, T0, 48),
         pltpu.SemaphoreType.DMA((3 + TILES,)),
-        pltpu.SemaphoreType.DMA((26,)),
-        pltpu.SemaphoreType.DMA((26,)),
+        pltpu.SemaphoreType.DMA((32,)),
+        pltpu.SemaphoreType.DMA((32,)),
     ]
     anywhere = pl.BlockSpec(memory_space=pl.ANY)
     return pl.pallas_call(

time: 36.4 us -> 34.9 us (0.959)
  Pallas kernels: 34.4 us -> 32.6 us
    pallas_call x1, Pallas kernels: 34.4 us -> 32.6 us  [local(): pl.pallas_call(kernel, out_shape=jax.ShapeDtypeStruct(target.shape, f32),...]
where the time goes in v3:
time: 34.9 us; the launch traced here: 34.3 us
  Pallas kernels  32.6 us (93%)
  local copies, waits for them, and re-layouts  1.62 us (5%)
    pallas_call x1, Pallas kernels, local(): pl.pallas_call(kernel, out_shape=jax.ShapeDtypeStruct(target.shape, f32),...  32.6 us
    unnamed x1, local copies, waits for them, and re-layouts  1.62 us

profile of v3, /device:TPU:6, one launch (start us, length us, event | category | flops | bytes accessed | tf_op | source)
XLA Modules:
  0.0 34.3 jit_solution(17561506155324164225)
XLA Ops:
  0.0 32.6 %vcycle.1 = f32[3,16,1024]{2,1,0:T(8,128)} custom-call(s32[3]{0:T(128)} %sweeps.1, f32[3,16,1024]{2,1,0:T(8,128)} %target.1, f32[2,3,16,1024]{3,2,1,0:T(8,128)} %grad_x.1, f32[2,3,16,1024]{3,2,1,0:T(8,128)} %grad_y.1, s32[16,1024]{1,0:T(8,128)} %labels.1), custom_call_target="tpu_custom_call" | custom-call | tf_op jit(solution)/shard_map/vcycle/pallas_call | solution.py:414
  32.6 1.6 %copy.7 = f32[3,16,1024]{2,1,0:T(8,128)} copy(f32[3,16,1024]{2,1,0:T(8,128)} %vcycle.1) | data formatting | bytes 393216

commit v4 on v3

--- a/solution.py
+++ b/solution.py
@@ -107,11 +107,11 @@
 
 
 def kernel(
-    sweeps, target, grad_x, grad_y, labels, out,
+    counts, target, grad_x, grad_y, labels, out,
     gx, gy, lab, v0, w0, b0, sy, sx, ny, ey, wy, wx, xn, xs, xnw, xsw,
     ps, pn, rn, rs, pe, pw, re, rw,
     b1, v1, w1, vp, wp, b2, v2, w2, zn, zs, un, us, hs, fn, fs, gn, gs, tmp,
-    in_sem, send, recv,
+    sweeps, in_sem, send, recv,
 ):
     lon, lat = lax.axis_index("lon"), lax.axis_index("lat")
     nlon, nlat = lax.axis_size("lon"), lax.axis_size("lat")
@@ -125,19 +125,27 @@
     for dlat, dlon in peers:
         pl.semaphore_signal(barrier, inc=1, device_id=peer(dlat, dlon), device_id_type=MESH)
 
-    loads = [
-        pltpu.make_async_copy(labels, lab, in_sem.at[0]),
-        pltpu.make_async_copy(grad_x, gx, in_sem.at[1]),
-        pltpu.make_async_copy(grad_y, gy, in_sem.at[2]),
-    ]
-    for t in range(TILES):
-        loads.append(
-            pltpu.make_async_copy(
-                target.at[:, :, pl.ds(t * L, L)], v0.at[:, t, pl.ds(O0, ROWS)], in_sem.at[3 + t]
-            )
-        )
-    for load in loads:
-        load.start()
+    loads = []
+
+    def load(src, dst):
+        loads.append(pltpu.make_async_copy(src, dst, in_sem.at[len(loads)]))
+
+    for tiles, cols in (((0,), pl.ds(0, L)), ((TILES - 1,), pl.ds((TILES - 2) * L, 2 * L))):
+        load(grad_x.at[:, :, :, cols], gx.at[:, :, :, cols])
+        load(grad_y.at[:, :, :, cols], gy.at[:, :, :, cols])
+        load(labels.at[:, cols], lab.at[:, cols])
+        for t in tiles:
+            load(target.at[:, :, pl.ds(t * L, L)], v0.at[:, t, pl.ds(O0, ROWS)])
+    edge_loads = len(loads)
+    cols = pl.ds(L, (TILES - 3) * L)
+    load(grad_x.at[:, :, :, cols], gx.at[:, :, :, cols])
+    load(grad_y.at[:, :, :, cols], gy.at[:, :, :, cols])
+    load(labels.at[:, cols], lab.at[:, cols])
+    for t in range(1, TILES - 1):
+        load(target.at[:, :, pl.ds(t * L, L)], v0.at[:, t, pl.ds(O0, ROWS)])
+    load(counts, sweeps)
+    for copy in loads:
+        copy.start()
 
     used = [0]
 
@@ -175,64 +183,50 @@
                 ref[c, t, 0:8] = jnp.zeros((8, L), jnp.float32)
                 ref[c, t, 24:32] = jnp.zeros((8, L), jnp.float32)
 
-    for load in loads[:3]:
-        load.wait()
+    for copy in loads[:edge_loads]:
+        copy.wait()
 
     def picked(ref, c, t, rows):
         cols = slice(t * L, (t + 1) * L)
         return jnp.where(lab[rows, cols] == 0, ref[0, c, rows, cols], ref[1, c, rows, cols])
 
-    for t in range(TILES):
+    def south_edge(t):
         edge = [rolled(picked(gy, c, t, slice(8, 16)), c + 1, 0) for c in range(CH)]
         sy[t] = jnp.where(sub == 0, edge[0], jnp.where(sub == 1, edge[1], edge[2]))[0:4]
-    edge = [rolled(picked(gx, c, TILES - 1, slice(0, ROWS)), c + 1, 1) for c in range(CH)]
-    sx[...] = jnp.where(lane == 0, edge[0], jnp.where(lane == 1, edge[1], edge[2]))
+
+    own = slice(O0, O0 + ROWS)
+    all_rows = slice(0, ROWS)
+
+    def right_side(c, t):
+        x = picked(gx, c, t, all_rows)
+        y = picked(gy, c, t, all_rows)
+        before = 0.0 if t == 0 else rolled(picked(gx, c, t - 1, all_rows), 1, 1)
+        west = jnp.where(first, before, rolled(x, 1, 1))
+        north = jnp.where(row == 0, 0.0, rolled(y, 1, 0))
+        v = v0[c, t, own]
+        b = screening * v - ((x - west) + (y - north))
+        b0[c, t, own] = b
+        vn, vs, bn, bs = v[0:8], v[8:16], b[0:8], b[8:16]
+        bs = bs + jnp.where(sub == 4, rolled(vs, 1, 0), 0.0)
+        ps[c, t] = jnp.where(upper, rolled(bs, 4, 0), vs)
+        bn = bn + jnp.where(sub == 3, rolled(vn, -1, 0), 0.0)
+        pn[c, t] = jnp.where(upper, vn, rolled(bn, 4, 0))
+        return v, b, x
+
+    east = []
+    for c in range(CH):
+        v, b, _ = right_side(c, 0)
+        pw[c] = jnp.where(low, v, rolled(b, L // 2, 1))
+        v, b, x = right_side(c, TILES - 1)
+        pe[c] = jnp.where(low, rolled(b, L // 2, 1), v)
+        east.append(rolled(x, c + 1, 1))
+    south_edge(0)
+    south_edge(TILES - 1)
+    sx[...] = jnp.where(lane == 0, east[0], jnp.where(lane == 1, east[1], east[2]))
 
     pl.semaphore_wait(barrier, len(peers))
     north8, south8 = pl.ds(0, 8), pl.ds(8, 8)
-    edges = [
-        remote(sy, ny.at[pl.ds(0, TILES)], 1, 0),
-        remote(sy.at[0], ny.at[TILES], 1, -1),
-        remote(sy.at[TILES - 1], ny.at[TILES + 1], 1, 1),
-        remote(sy.at[0], ey, 0, -1),
-        remote(sy.at[TILES - 1], wy, 0, 1),
-        remote(sx, wx, 0, 1),
-        remote(sx.at[north8], xs, -1, 0),
-        remote(sx.at[south8], xn, 1, 0),
-        remote(sx.at[north8], xsw, -1, 1),
-        remote(sx.at[south8], xnw, 1, 1),
-    ]
-    for copy in edges:
-        copy.start()
-    for load in loads[3:]:
-        load.wait()
-
-    own = slice(O0, O0 + ROWS)
-    for c in range(CH):
-        before = None
-        for t in range(TILES):
-            x = picked(gx, c, t, slice(0, ROWS))
-            y = picked(gy, c, t, slice(0, ROWS))
-            moved = rolled(x, 1, 1)
-            west = jnp.where(first, 0.0 if t == 0 else before, moved)
-            before = moved
-            north = jnp.where(row == 0, 0.0, rolled(y, 1, 0))
-            v = v0[c, t, own]
-            b = screening * v - ((x - west) + (y - north))
-            b0[c, t, own] = b
-            vn, vs, bn, bs = v[0:8], v[8:16], b[0:8], b[8:16]
-            bs = bs + jnp.where(sub == 4, rolled(vs, 1, 0), 0.0)
-            ps[c, t] = jnp.where(upper, rolled(bs, 4, 0), vs)
-            bn = bn + jnp.where(sub == 3, rolled(vn, -1, 0), 0.0)
-            pn[c, t] = jnp.where(upper, vn, rolled(bn, 4, 0))
-            if t == 0:
-                pw[c] = jnp.where(low, v, rolled(b, L // 2, 1))
-            if t == TILES - 1:
-                pe[c] = jnp.where(low, rolled(b, L // 2, 1), v)
-
     e0 = [
-        remote(ps, rn.at[:, pl.ds(0, TILES)], 1, 0),
-        remote(pn, rs.at[:, pl.ds(0, TILES)], -1, 0),
         remote(pe, rw, 0, 1),
         remote(pw, re, 0, -1),
         remote(ps.at[:, TILES - 1], rn.at[:, TILES + 1], 1, 1),
@@ -240,8 +234,37 @@
         remote(pn.at[:, TILES - 1], rs.at[:, TILES + 1], -1, 1),
         remote(pn.at[:, 0], rs.at[:, TILES], -1, -1),
     ]
-    for copy in e0:
+    edges = [
+        remote(sx, wx, 0, 1),
+        remote(sy.at[0], ey, 0, -1),
+        remote(sy.at[TILES - 1], wy, 0, 1),
+        remote(sy.at[0], ny.at[TILES], 1, -1),
+        remote(sy.at[TILES - 1], ny.at[TILES + 1], 1, 1),
+        remote(sx.at[north8], xsw, -1, 1),
+        remote(sx.at[south8], xnw, 1, 1),
+        remote(sx.at[north8], xs, -1, 0),
+        remote(sx.at[south8], xn, 1, 0),
+    ]
+    for copy in e0 + edges:
         copy.start()
+
+    for copy in loads[edge_loads:]:
+        copy.wait()
+    for t in range(1, TILES - 1):
+        south_edge(t)
+    to_south = remote(sy, ny.at[pl.ds(0, TILES)], 1, 0)
+    to_south.start()
+    edges.append(to_south)
+    for c in range(CH):
+        for t in range(1, TILES - 1):
+            right_side(c, t)
+    along = [
+        remote(ps, rn.at[:, pl.ds(0, TILES)], 1, 0),
+        remote(pn, rs.at[:, pl.ds(0, TILES)], -1, 0),
+    ]
+    for copy in along:
+        copy.start()
+    e0 += along
 
     inside0 = inside(0, -8, R0)
     has_north = jnp.where(lat > 0, 1.0, 0.0).astype(jnp.float32)
@@ -406,15 +429,16 @@
         vmem(R1),
         vmem(T1, 8), vmem(T1, 8), vmem(T1, 8), vmem(T1, 8),
         vmem(CH, T0, 48),
-        pltpu.SemaphoreType.DMA((3 + TILES,)),
+        pltpu.SMEM((LEVELS,), jnp.int32),
+        pltpu.SemaphoreType.DMA((18,)),
         pltpu.SemaphoreType.DMA((32,)),
         pltpu.SemaphoreType.DMA((32,)),
     ]
     anywhere = pl.BlockSpec(memory_space=pl.ANY)
     return pl.pallas_call(
         kernel,
-        out_shape=jax.ShapeDtypeStruct(target.shape, f32),
-        in_specs=[pl.BlockSpec(memory_space=pltpu.SMEM)] + [anywhere] * 4,
+        out_shape=pltpu.VMEM(target.shape, f32),
+        in_specs=[anywhere] * 5,
         out_specs=pl.BlockSpec(memory_space=pltpu.VMEM),
         scratch_shapes=scratch,
         compiler_params=pltpu.CompilerParams(collective_id=0, has_side_effects=True),

time: 34.9 us -> 31.2 us (0.89); the launches traced: 34.3 us -> 31.1 us
  Pallas kernels: 32.6 us -> 30.4 us
  local copies, waits for them, and re-layouts: 1.62 us -> 0.68 us
    pallas_call x1, Pallas kernels: 32.6 us -> 30.4 us  [local(): pl.pallas_call(kernel, out_shape=pltpu.VMEM(target.shape, f32), in_specs=...]
    unnamed x1, local copies, waits for them, and re-layouts: 1.62 us -> 0.68 us
where the time goes in v4:
time: 31.2 us; the launch traced here: 31.1 us
  Pallas kernels  30.4 us (97%)
  local copies, waits for them, and re-layouts  0.68 us (2%)
    pallas_call x1, Pallas kernels, local(): pl.pallas_call(kernel, out_shape=pltpu.VMEM(target.shape, f32), in_specs=...  30.4 us
    unnamed x1, local copies, waits for them, and re-layouts  0.68 us

profile of v4, /device:TPU:6, one launch (start us, length us, event | category | flops | bytes accessed | tf_op | source)
XLA Modules:
  0.0 31.1 jit_solution(6476446201120721835)
XLA Ops:
  0.0 30.4 %vcycle.1 = f32[3,16,1024]{2,1,0:T(8,128)S(1)} custom-call(s32[3]{0:T(128)} %counts.1, f32[3,16,1024]{2,1,0:T(8,128)} %target.1, f32[2,3,16,1024]{3,2,1,0:T(8,128)} %grad_x.1, f32[2,3,16,1024]{3,2,1,0:T(8,128)} %grad_y.1, s32[16,1024]{1,0:T(8,128)} %labels.1), custom_call_target="tpu_custom_call" | custom-call | tf_op jit(solution)/shard_map/vcycle/pallas_call | solution.py:438
  30.4 0.7 %copy.7 = f32[3,16,1024]{2,1,0:T(8,128)} copy(f32[3,16,1024]{2,1,0:T(8,128)S(1)} %vcycle.1) | data formatting | bytes 393216

commit v5 on v4

--- a/solution.py
+++ b/solution.py
@@ -62,20 +62,23 @@
             dst[c, t, at : at + rows] = x + factor * r
 
 
-def restrict(src, rhs, dst, tmp, tiles, at, rhs_at, rows, dst_at, count, scale):
+def restrict(src, rhs, dst, tmp, tiles, at, rhs_at, rows, dst_at, count, scale, which):
     low = lanes_of(count)[2]
     pick = (2 * iota(count, 1)) % L
     for c in range(CH):
-        for t in range(tiles):
+        parts = {}
+        fine = [t for k in which for t in (2 * k, 2 * k + 1) if t < tiles]
+        for t in fine:
             tmp[c, t, 0:rows] = residual(src, rhs, c, t, tiles, at, rhs_at, rows, scale)[1]
-        parts = []
-        for t in range(tiles):
+        for t in fine:
             pair = tmp[c, t, pl.ds(0, count, stride=2)] + tmp[c, t, pl.ds(1, count, stride=2)]
             pair = pair + rolled(pair, -1, 1)
-            parts.append(0.25 * jnp.take_along_axis(pair, pick, axis=1))
-        for t in range(tiles // 2):
-            dst[c, t, dst_at : dst_at + count] = jnp.where(low, parts[2 * t], parts[2 * t + 1])
-        dst[c, tiles // 2, dst_at : dst_at + count] = parts[-1]
+            parts[t] = 0.25 * jnp.take_along_axis(pair, pick, axis=1)
+        for k in which:
+            x = parts[2 * k]
+            if 2 * k + 1 < tiles:
+                x = jnp.where(low, x, parts[2 * k + 1])
+            dst[c, k, dst_at : dst_at + count] = x
 
 
 def prolong_rows(src, c, tiles, at, rows, tmp):
@@ -110,7 +113,7 @@
     counts, target, grad_x, grad_y, labels, out,
     gx, gy, lab, v0, w0, b0, sy, sx, ny, ey, wy, wx, xn, xs, xnw, xsw,
     ps, pn, rn, rs, pe, pw, re, rw,
-    b1, v1, w1, vp, wp, b2, v2, w2, zn, zs, un, us, hs, fn, fs, gn, gs, tmp,
+    vi, wi, b1, v1, w1, vp, wp, b2, v2, w2, zn, zs, un, us, hs, fn, fs, gn, gs, tmp,
     sweeps, in_sem, send, recv,
 ):
     lon, lat = lax.axis_index("lon"), lax.axis_index("lat")
@@ -254,7 +257,6 @@
         south_edge(t)
     to_south = remote(sy, ny.at[pl.ds(0, TILES)], 1, 0)
     to_south.start()
-    edges.append(to_south)
     for c in range(CH):
         for t in range(1, TILES - 1):
             right_side(c, t)
@@ -264,44 +266,56 @@
     ]
     for copy in along:
         copy.start()
-    e0 += along
 
     inside0 = inside(0, -8, R0)
     has_north = jnp.where(lat > 0, 1.0, 0.0).astype(jnp.float32)
-    for copy in edges:
-        copy.wait()
-
     def column(x, c):
         return jnp.where(first if x.shape[0] == ROWS else first8, rolled(x, -c, 1), 0.0)
 
     def line(x, c):
         return jnp.where(sub == 0, x[c : c + 1], 0.0)
 
-    for c in range(CH):
-        b0[c, 0, own] = b0[c, 0, own] + column(wx[...], c)
+    for copy in along + [to_south]:
+        copy.wait()
+    for c in range(CH):
         for t in range(TILES):
             b0[c, t, 8:16] = b0[c, t, 8:16] + has_north * line(ny[t], c)
-
-    for copy in e0:
-        copy.wait()
-
-    for c in range(CH):
-        halves = [(rn[c, t], rs[c, t]) for t in range(TILES)]
-        halves.append(
-            (jnp.where(low8, rn[c, TILES], rn[c, TILES + 1]), jnp.where(low8, rs[c, TILES], rs[c, TILES + 1]))
-        )
-        for t, (n, s) in enumerate(halves):
+            n, s = rn[c, t], rs[c, t]
             v0[c, t, 0:8] = jnp.where(upper, 0.0, n) * inside0[0:8]
             v0[c, t, 24:32] = jnp.where(upper, s, 0.0) * inside0[24:32]
-            n, s = rolled(n, 4, 0), rolled(s, 4, 0)
-            below = sy[t] if t < TILES else jnp.where(low4, ey[...], wy[...])
-            s = s + line(below, c)
-            if t == 0:
-                n, s = n + column(xnw[...], c), s + column(xsw[...], c)
-            if t == TILES:
-                n, s = n + column(xn[...], c), s + column(xs[...], c)
-            b0[c, t, 0:8] = n
-            b0[c, t, 24:32] = s
+            b0[c, t, 0:8] = rolled(n, 4, 0)
+            b0[c, t, 24:32] = rolled(s, 4, 0) + line(sy[t], c)
+
+    f0 = [inside0[4:28] * step(0, i) for i in range(MAXS)]
+    inner = (1, 2)
+    for i in range(MAXS):
+        a, b = ((v0, wi), (wi, vi), (vi, wi), (wi, vi))[i]
+        sweep(a, b, b0, TILES, 4, 4, 24, f0[i], 1.0)
+    restrict(vi, b0, b1, tmp, TILES, O0, O0, ROWS, O1, 8, 1.0, inner)
+    rows1 = pl.ds(O1, 8)
+
+    def there(d):
+        return pl.ds(O1 - 8 * d, 8)
+
+    e1 = [
+        remote(b1.at[:, pl.ds(1, 2), rows1], b1.at[:, pl.ds(1, 2), there(d)], d, 0) for d in (2, -2, 1, -1)
+    ]
+    for copy in e1:
+        copy.start()
+
+    for copy in edges + e0:
+        copy.wait()
+    for c in range(CH):
+        b0[c, 0, own] = b0[c, 0, own] + column(wx[...], c)
+        b0[c, 0, 0:8] = b0[c, 0, 0:8] + column(xnw[...], c)
+        b0[c, 0, 24:32] = b0[c, 0, 24:32] + column(xsw[...], c)
+        n = jnp.where(low8, rn[c, TILES], rn[c, TILES + 1])
+        s = jnp.where(low8, rs[c, TILES], rs[c, TILES + 1])
+        v0[c, TILES, 0:8] = jnp.where(upper, 0.0, n) * inside0[0:8]
+        v0[c, TILES, 24:32] = jnp.where(upper, s, 0.0) * inside0[24:32]
+        s = rolled(s, 4, 0) + line(jnp.where(low4, ey[...], wy[...]), c)
+        b0[c, TILES, 0:8] = rolled(n, 4, 0) + column(xn[...], c)
+        b0[c, TILES, 24:32] = s + column(xs[...], c)
         v0[c, TILES, own] = jnp.where(low, re[c], rw[c])
         b = rolled(jnp.where(low, rw[c], re[c]), L // 2, 1) + column(sx[...], c)
         above = has_north * line(jnp.where(low4, ny[TILES], ny[TILES + 1]), c)
@@ -310,9 +324,9 @@
 
     for i in range(MAXS):
         a, b = (v0, w0) if i % 2 == 0 else (w0, v0)
-        sweep(a, b, b0, T0, 4, 4, 24, inside0[4:28] * step(0, i), 1.0)
-
-    restrict(v0, b0, b1, tmp, T0, O0, O0, ROWS, O1, 8, 1.0)
+        sweep(a, b, b0, T0, 4, 4, 24, f0[i], 1.0)
+
+    restrict(v0, b0, b1, tmp, T0, O0, O0, ROWS, O1, 8, 1.0, (0, 3, 4))
     for t in range(T1):
         rows = [b1[c, t, O1 : O1 + 8] for c in range(CH)]
         n, s = ([rolled(x, 2 * c + k, 0) for c, x in enumerate(rows)] for k in (0, 2))
@@ -322,21 +336,22 @@
     hs[O1 : O1 + 8] = jnp.where(lane8 < 2 * WIDE, turned[0], jnp.where(lane8 < 4 * WIDE, turned[1], turned[2]))
 
     def sent(d):
-        rows, there = pl.ds(O1, 8), pl.ds(O1 - 8 * d, 8)
         return [
-            remote(b1.at[:, pl.ds(0, T1 - 1), rows], b1.at[:, pl.ds(0, T1 - 1), there], d, 0),
-            remote(hs.at[rows], hs.at[there], d, 0),
+            remote(b1.at[:, 0, rows1], b1.at[:, 0, there(d)], d, 0),
+            remote(b1.at[:, 3, rows1], b1.at[:, 3, there(d)], d, 0),
+            remote(hs.at[rows1], hs.at[there(d)], d, 0),
         ]
 
-    e1 = sent(2) + sent(-2)
-    e1 += [remote(fs, gn, 3, 0), remote(fn, gs, -3, 0)]
-    e1 += sent(1) + sent(-1)
+    late = sent(2) + sent(-2)
+    late += [remote(fs, gn, 3, 0), remote(fn, gs, -3, 0)]
+    late += sent(1) + sent(-1)
     e2 = [
         remote(un, zs, -1, 0),
         remote(us, zn, 1, 0),
     ]
-    for copy in e1:
-        copy.start()
+    for copy in late:
+        copy.start()
+    e1 += late
     for c in range(CH):
         for t in range(T0):
             un[c, t] = v0[c, t, O0 : O0 + 4]
@@ -366,7 +381,7 @@
     for c in range(CH):
         for t in range(T1):
             tmp[c, t, 40:48] = jnp.zeros((8, L), jnp.float32)
-    restrict(w1, b1, b2, tmp, T1, 8, 8, 40, 0, R2, 0.25)
+    restrict(w1, b1, b2, tmp, T1, 8, 8, 40, 0, R2, 0.25, range(T2))
 
     f = factor(2, 0, O2, 0, R2)
     for c in range(CH):
@@ -397,7 +412,7 @@
             v0[c, t, 24:28] = (zs[c, t] + fine[t][24:28]) * inside0[24:28]
     for i in range(MAXS - 1):
         a, b = (v0, w0) if i % 2 == 0 else (w0, v0)
-        sweep(a, b, b0, T0, 4, 4, 24, inside0[4:28] * step(0, i), 1.0)
+        sweep(a, b, b0, T0, 4, 4, 24, f0[i], 1.0)
     f = step(0, MAXS - 1)
     for c in range(CH):
         for t in range(TILES):
@@ -422,6 +437,7 @@
         vmem(CH, TILES, 8), vmem(CH, TILES, 8),
         vmem(CH, TILES + 2, 8), vmem(CH, TILES + 2, 8),
         vmem(CH, ROWS), vmem(CH, ROWS), vmem(CH, ROWS), vmem(CH, ROWS),
+        vmem(CH, TILES, R0), vmem(CH, TILES, R0),
         vmem(CH, T1, R1), vmem(CH, T1, R1), vmem(CH, T1, R1),
         vmem(CH, T1, RP), vmem(CH, T1, RP),
         vmem(CH, T2, R2), vmem(CH, T2, R2), vmem(CH, T2, R2),
@@ -431,8 +447,8 @@
         vmem(CH, T0, 48),
         pltpu.SMEM((LEVELS,), jnp.int32),
         pltpu.SemaphoreType.DMA((18,)),
-        pltpu.SemaphoreType.DMA((32,)),
-        pltpu.SemaphoreType.DMA((32,)),
+        pltpu.SemaphoreType.DMA((40,)),
+        pltpu.SemaphoreType.DMA((40,)),
     ]
     anywhere = pl.BlockSpec(memory_space=pl.ANY)
     return pl.pallas_call(

time: 31.2 us -> 31.2 us (level)
  the two profiles are of different devices: /device:TPU:6 before, /device:TPU:2 now
where the time goes in v5:
time: 31.2 us; the launch traced here: 31.1 us
  Pallas kernels  30.4 us (97%)
  local copies, waits for them, and re-layouts  0.68 us (2%)
    pallas_call x1, Pallas kernels, local(): pl.pallas_call(kernel, out_shape=pltpu.VMEM(target.shape, f32), in_specs=...  30.4 us
    unnamed x1, local copies, waits for them, and re-layouts  0.68 us

profile of v5, /device:TPU:2, one launch (start us, length us, event | category | flops | bytes accessed | tf_op | source)
XLA Modules:
  0.0 31.1 jit_solution(5959182248185539425)
XLA Ops:
  0.0 30.4 %vcycle.1 = f32[3,16,1024]{2,1,0:T(8,128)S(1)} custom-call(s32[3]{0:T(128)} %counts.1, f32[3,16,1024]{2,1,0:T(8,128)} %target.1, f32[2,3,16,1024]{3,2,1,0:T(8,128)} %grad_x.1, f32[2,3,16,1024]{3,2,1,0:T(8,128)} %grad_y.1, s32[16,1024]{1,0:T(8,128)} %labels.1), custom_call_target="tpu_custom_call" | custom-call | tf_op jit(solution)/shard_map/vcycle/pallas_call | solution.py:454
  30.4 0.7 %copy.7 = f32[3,16,1024]{2,1,0:T(8,128)} copy(f32[3,16,1024]{2,1,0:T(8,128)S(1)} %vcycle.1) | data formatting | bytes 393216

commit v6 on v5

--- a/solution.py
+++ b/solution.py
@@ -444,7 +444,7 @@
         vmem(CH, T0, 4), vmem(CH, T0, 4), vmem(CH, T0, 4), vmem(CH, T0, 4),
         vmem(R1),
         vmem(T1, 8), vmem(T1, 8), vmem(T1, 8), vmem(T1, 8),
-        vmem(CH, T0, 48),
+        vmem(CH, T0, 56),
         pltpu.SMEM((LEVELS,), jnp.int32),
         pltpu.SemaphoreType.DMA((18,)),
         pltpu.SemaphoreType.DMA((40,)),

time: 31.2 us -> 31.2 us (level)
  no operation moved by 1% of the time
where the time goes in v6:
time: 31.2 us; the launch traced here: 31.1 us
  Pallas kernels  30.4 us (97%)
  local copies, waits for them, and re-layouts  0.68 us (2%)
    pallas_call x1, Pallas kernels, local(): pl.pallas_call(kernel, out_shape=pltpu.VMEM(target.shape, f32), in_specs=...  30.4 us
    unnamed x1, local copies, waits for them, and re-layouts  0.68 us

profile of v6, /device:TPU:2, one launch (start us, length us, event | category | flops | bytes accessed | tf_op | source)
XLA Modules:
  0.0 31.1 jit_solution(14507665189680500206)
XLA Ops:
  0.0 30.4 %vcycle.1 = f32[3,16,1024]{2,1,0:T(8,128)S(1)} custom-call(s32[3]{0:T(128)} %counts.1, f32[3,16,1024]{2,1,0:T(8,128)} %target.1, f32[2,3,16,1024]{3,2,1,0:T(8,128)} %grad_x.1, f32[2,3,16,1024]{3,2,1,0:T(8,128)} %grad_y.1, s32[16,1024]{1,0:T(8,128)} %labels.1), custom_call_target="tpu_custom_call" | custom-call | tf_op jit(solution)/shard_map/vcycle/pallas_call | solution.py:454
  30.4 0.7 %copy.7 = f32[3,16,1024]{2,1,0:T(8,128)} copy(f32[3,16,1024]{2,1,0:T(8,128)S(1)} %vcycle.1) | data formatting | bytes 393216
